TPU v7x, 32 devices: a whole 2x2x4 slice. The times are simulated.
32 devices in a mesh: dp: 8 (over y, x, core), mp: 4 (over z).
Axes of the slice: x: 2, y: 2, z: 4, core: 2. Of those that a mesh axis runs over, the one named last changes fastest.
Arguments:
- states: bfloat16 [128, 80, 768], P('dp'), may hold values from -6 to 6
- hist_len: int32 [128], P('dp'), may hold values from 1 to 20
- norm_gain: float32 [768], replicated, may hold values from 0.5 to 1.5
- qkv_weight: bfloat16 [768, 3, 12, 64], P(None, None, 'mp'), may hold values from -1 to 1
- output_weight: bfloat16 [12, 64, 768], P('mp'), may hold values from -0.21875 to 0.21875
- cotangent: bfloat16 [128, 80, 768], P('dp'), may hold values from -6 to 6
Outputs:
- attended: bfloat16 [128, 80, 768], P('dp')
- grad_states: bfloat16 [128, 80, 768], P('dp')
- grad_qkv: float32 [768, 3, 12, 64], P('dp', None, 'mp')
- output_weight_gradient: float32 [12, 64, 768], P('mp', None, 'dp')
- grad_gain: float32 [768], P('dp')
All inputs are finite; a program needn't handle non-finite values.
Results may differ from a plain program's by a relative error of at most 0.012.
Values may be sent and summed in bfloat16 or wider, within the bound.
No kernel may reach another device: no remote copies, remote signals or barrier semaphores. Data moves between devices by JAX's collectives and lax.ppermute only.
A program may use at most 128 MiB of HBM per device.

v0:
```python
import functools

import jax
import jax.numpy as jnp
from jax import lax
from jax.experimental import pallas as pl
from jax.experimental.pallas import tpu as pltpu
from jax.sharding import PartitionSpec as P


LEVELS = 4
EPS = 1e-06
F32 = jnp.float32
BF16 = jnp.bfloat16


def dot_nt(a, b):
    return lax.dot_general(a, b, (((1,), (1,)), ((), ())), preferred_element_type=F32)


def dot_nn(a, b):
    return lax.dot_general(a, b, (((1,), (0,)), ((), ())), preferred_element_type=F32)


def dot_tn(a, b):
    return lax.dot_general(a, b, (((0,), (0,)), ((), ())), preferred_element_type=F32)


def attention(q, k, v, g, valid, heads, width):
    seq = q.shape[0]
    lane_head = lax.broadcasted_iota(jnp.int32, (1, heads * width), 1) // width
    masks = [(lane_head == h).astype(BF16) for h in range(heads)]
    q_blocks = jnp.concatenate([q * m for m in masks], axis=0)
    g_blocks = jnp.concatenate([g * m for m in masks], axis=0)
    scores = dot_nt(k, q_blocks)
    row = lax.broadcasted_iota(jnp.int32, scores.shape, 0)
    scores = jnp.where(row < valid, scores, -1e30)
    top = jnp.max(scores, axis=0, keepdims=True)
    exp_scores = jnp.exp(scores - top)
    prob = exp_scores * (1.0 / jnp.sum(exp_scores, axis=0, keepdims=True))
    prob_bf = prob.astype(BF16)
    grad_prob = dot_nt(v, g_blocks)
    delta = jnp.sum(prob * grad_prob, axis=0, keepdims=True)
    grad_scores = (prob * (grad_prob - delta)).astype(BF16)
    grad_v = dot_nn(prob_bf, g_blocks)
    grad_k = dot_nn(grad_scores, q_blocks)

    def diagonal(full):
        out = full[:seq]
        for h in range(1, heads):
            out = jnp.where(lane_head == h, full[h * seq : (h + 1) * seq], out)
        return out

    context = diagonal(dot_tn(prob_bf, v))
    grad_q = diagonal(dot_tn(grad_scores, k))
    return grad_q, grad_k, grad_v, context


def keep_rows(len_ref, first, count, seq):
    rows = [lax.broadcasted_iota(jnp.int32, (seq, 1), 0) < LEVELS * len_ref[first + b] for b in range(count)]
    return jnp.concatenate([r.astype(F32) for r in rows], axis=0)


def shard_body(len_ref, normed, mcot, w_q, w_k, w_v, w_o, out_ref, scratch, seq, heads, width):
    q_s, k_s, v_s, g_s = scratch
    chunk = pl.program_id(0)
    count = normed.shape[0] // seq
    q_s[...] = dot_nt(normed, w_q).astype(BF16)
    k_s[...] = dot_nt(normed, w_k).astype(BF16)
    v_s[...] = dot_nt(normed, w_v).astype(BF16)
    g_s[...] = dot_nt(mcot, w_o).astype(BF16)
    for b in range(count):
        rows = slice(b * seq, (b + 1) * seq)
        valid = LEVELS * len_ref[chunk * count + b]
        parts = attention(q_s[rows], k_s[rows], v_s[rows], g_s[rows], valid, heads, width)
        for n, part in enumerate(parts):
            out_ref[n, rows] = part.astype(BF16)


def own_kernel(seq, heads, width, len_ref, states_ref, cot_ref, gain_ref, qkv_ref, wo_ref,
               normed_ref, mcot_ref, out_ref, *scratch):
    wide = states_ref[...].astype(F32)
    inv = lax.rsqrt(jnp.mean(wide * wide, axis=-1, keepdims=True) + EPS)
    normed = (wide * inv * gain_ref[...]).astype(BF16)
    normed_ref[...] = normed
    count = normed.shape[0] // seq
    keep = keep_rows(len_ref, pl.program_id(0) * count, count, seq)
    mcot = (cot_ref[...].astype(F32) * keep).astype(BF16)
    mcot_ref[...] = mcot
    n = heads * width
    shard_body(len_ref, normed, mcot, qkv_ref[:n], qkv_ref[n : 2 * n], qkv_ref[2 * n : 3 * n], wo_ref[...],
               out_ref.at[:], scratch, seq, heads, width)


def far_kernel(seq, heads, width, parts, len_ref, meta_ref, normed_ref, mcot_ref, *refs):
    blocks = refs[:parts]
    out_ref, wt_ref, q_s, k_s, v_s, g_s, sems = refs[parts:]
    n = heads * width
    size = 4 * n // parts

    @pl.when(pl.program_id(0) == 0)
    def _():
        copies = []
        for r in range(parts):
            place = pl.multiple_of((meta_ref[1] ^ r) * size, 8)
            copies.append(pltpu.make_async_copy(blocks[r], wt_ref.at[pl.ds(place, size)], sems.at[r]))
        for copy in copies:
            copy.start()
        for copy in copies:
            copy.wait()

    w = [wt_ref[i * n : (i + 1) * n] for i in range(4)]
    shard_body(len_ref, normed_ref[...], mcot_ref[...], w[0], w[1], w[2], w[3],
               out_ref.at[:], (q_s, k_s, v_s, g_s), seq, heads, width)


def weight_grad_kernel(parts, n, meta_ref, normed_ref, mcot_ref, all_ref, *refs):
    outs, acc = refs[:-1], refs[-1]
    step = pl.program_id(0)
    rows = normed_ref.shape[1]
    size = rows * pl.num_programs(0) // parts
    per = parts // 2
    for i in range(4):
        left = mcot_ref[...] if i == 3 else normed_ref[...]
        piece = dot_tn(left, all_ref[i])
        for c in range(per):
            acc[i, step * per + c] = piece[c * size : (c + 1) * size]

    @pl.when(step == pl.num_programs(0) - 1)
    def _():
        for r in range(parts):
            for i in range(4):
                value = acc[i, meta_ref[1] ^ r]
                if r % 2 == 0:
                    outs[r // 2][:, i * n : (i + 1) * n] = value
                else:
                    outs[per][r // 2, :, i * n : (i + 1) * n] = value.astype(BF16)


def final_kernel(seq, heads, width, parts, shards, len_ref, meta_ref, states_ref, normed_ref, mcot_ref, gain_ref,
                 all0_ref, all1_ref, qkv_ref, wo_ref, wt1_ref, *refs):
    blocks = refs[:parts]
    att_ref, grad_ref, gain_out_ref, wt_s, all_s = refs[parts : parts + 5]
    scratch, sems = refs[parts + 5 : -1], refs[-1]
    n = heads * width
    size = 4 * n // parts
    own = meta_ref[0]

    @pl.when(pl.program_id(0) == 0)
    def _():
        copies = [
            pltpu.make_async_copy(qkv_ref, wt_s.at[own, pl.ds(0, 3 * n)], sems.at[0]),
            pltpu.make_async_copy(wo_ref, wt_s.at[own, pl.ds(3 * n, n)], sems.at[1]),
            pltpu.make_async_copy(wt1_ref, wt_s.at[own ^ 1], sems.at[2]),
        ]
        for k in range(2, shards):
            for r in range(parts):
                place = pl.multiple_of((meta_ref[1] ^ r) * size, 8)
                copies.append(pltpu.make_async_copy(
                    blocks[r].at[k - 2], wt_s.at[own ^ k, pl.ds(place, size)], sems.at[3 + (k - 2) * parts + r]))
        for copy in copies:
            copy.start()
        for copy in copies:
            copy.wait()
        gain_out_ref[...] = jnp.zeros_like(gain_out_ref)

    all_s[own] = all0_ref[...]
    all_s[own ^ 1] = all1_ref[...]
    normed, mcot = normed_ref[...], mcot_ref[...]
    for k in range(2, shards):
        w = [wt_s[own ^ k, i * n : (i + 1) * n] for i in range(4)]
        shard_body(len_ref, normed, mcot, w[0], w[1], w[2], w[3],
                   all_s.at[own ^ k], scratch[4 * (k % 2) : 4 * (k % 2) + 4], seq, heads, width)
    total = None
    grad = None
    for s in range(shards):
        piece = dot_nn(all_s[s, 3], wt_s[s, 3 * n :])
        total = piece if total is None else total + piece
    wide = states_ref[...].astype(F32)
    att_ref[...] = (wide + total).astype(BF16)
    for s in range(shards):
        for i in range(3):
            piece = dot_nn(all_s[s, i], wt_s[s, i * n : (i + 1) * n])
            grad = piece if grad is None else grad + piece
    inv = lax.rsqrt(jnp.mean(wide * wide, axis=-1, keepdims=True) + EPS)
    unit = wide * inv
    gain_out_ref[...] += jnp.sum(grad * unit, axis=0, keepdims=True)
    unit_grad = grad * gain_ref[...]
    corr = jnp.mean(unit_grad * unit, axis=-1, keepdims=True)
    grad_ref[...] = (mcot.astype(F32) + inv * (unit_grad - unit * corr)).astype(BF16)


def body(dp, mp, states, hist_len, norm_gain, qkv_weight, output_weight, cotangent):
    batch, seq, d = states.shape
    _, _, heads, width = qkv_weight.shape
    n = heads * width
    rows = batch * seq
    parts = 8
    low = dp // parts
    i_hi = lax.axis_index("dp") // low
    i_mp = lax.axis_index("mp")
    meta = jnp.stack([i_mp, i_hi]).astype(jnp.int32)

    def hop_dp(x, r):
        return lax.ppermute(x, "dp", [(i, i ^ (r * low)) for i in range(dp)])

    def hop_mp(x, k):
        return lax.ppermute(x, "mp", [(i, i ^ k) for i in range(mp)])

    qkv_rows = jnp.transpose(qkv_weight, (1, 2, 3, 0)).reshape(3 * n, d)
    wo_rows = output_weight.reshape(n, d)
    size = 4 * n // parts
    mine = lax.dynamic_slice_in_dim(jnp.concatenate([qkv_rows, wo_rows], axis=0), i_hi * size, size, 0)

    first = [hop_mp(mine, k) for k in range(1, mp)]

    def spread(block):
        even = {0: block}
        for r in range(2, parts, 2):
            even[r] = hop_dp(block, r)
        blocks = dict(even)
        for r in range(0, parts, 2):
            blocks[r ^ 1] = hop_dp(even[r], 1)
        return [blocks[r] for r in range(parts)]

    near = spread(first[0])
    rest = spread(jnp.stack(first[1:]))

    flat_states = states.reshape(rows, d)
    flat_cot = cotangent.reshape(rows, d)
    gain = norm_gain.reshape(1, d)
    chunk = rows // 4
    grid = rows // chunk
    scratch = [pltpu.VMEM((chunk, n), BF16) for _ in range(4)]
    flops_in = 2 * rows * d * 4 * n
    row_spec = pl.BlockSpec((chunk, d), lambda c, *_: (c, 0))
    all_spec = pl.BlockSpec((4, chunk, n), lambda c, *_: (0, c, 0))
    any_spec = pl.BlockSpec(memory_space=pl.ANY)
    all_shape = jax.ShapeDtypeStruct((4, rows, n), BF16)
    row_shape = jax.ShapeDtypeStruct((rows, d), BF16)

    def whole(shape):
        return pl.BlockSpec(shape, lambda c, *_: tuple(0 for _ in shape))

    def call(kernel, flops, vmem, scalars, steps, in_specs, out_specs, out_shape, scratch_shapes):
        return pl.pallas_call(
            kernel, out_shape=out_shape,
            grid_spec=pltpu.PrefetchScalarGridSpec(
                num_scalar_prefetch=scalars, grid=(steps,), in_specs=in_specs, out_specs=out_specs,
                scratch_shapes=scratch_shapes),
            compiler_params=pltpu.CompilerParams(
                dimension_semantics=("arbitrary",), vmem_limit_bytes=vmem * 1024 * 1024),
            cost_estimate=pl.CostEstimate(flops=flops, bytes_accessed=rows * d * 8, transcendentals=0))

    normed, mcot, all0 = call(
        functools.partial(own_kernel, seq, heads, width), 3 * flops_in, 24, 1, grid,
        [row_spec, row_spec, whole((1, d)), whole((3 * n, d)), whole((n, d))],
        [row_spec, row_spec, all_spec], [row_shape, row_shape, all_shape], scratch,
    )(hist_len, flat_states, flat_cot, gain, qkv_rows, wo_rows)

    piece = (d // parts, 4 * n)
    half = parts // 2
    *kept, sent = call(
        functools.partial(weight_grad_kernel, parts, n), flops_in, 32, 1, 2,
        [pl.BlockSpec((rows, d // 2), lambda c, *_: (0, c))] * 2 + [whole((4, rows, n))],
        [whole(piece)] * half + [whole((half,) + piece)],
        [jax.ShapeDtypeStruct(piece, F32)] * half + [jax.ShapeDtypeStruct((half,) + piece, BF16)],
        [pltpu.VMEM((4, parts, d // parts, n), F32)],
    )(meta, normed, mcot, all0)
    pair = hop_dp(sent, 1)
    kept = [kept[r] + pair[r].astype(F32) for r in range(half)]
    arrived = [hop_dp(kept[r].astype(BF16), 2 * r) for r in range(1, half)]

    all1, wt1 = call(
        functools.partial(far_kernel, seq, heads, width, parts), 3 * flops_in, 24, 2, grid,
        [row_spec, row_spec] + [any_spec] * parts,
        [all_spec, whole((4 * n, d))], [all_shape, jax.ShapeDtypeStruct((4 * n, d), BF16)],
        scratch + [pltpu.SemaphoreType.DMA((parts,))],
    )(hist_len, meta, normed, mcot, *near)

    attended, grad_states, gain_part = call(
        functools.partial(final_kernel, seq, heads, width, parts, mp), 10 * flops_in, 44, 2, grid,
        [row_spec, row_spec, row_spec, whole((1, d)), all_spec, all_spec] + [any_spec] * (3 + parts),
        [row_spec, row_spec, whole((1, d))], [row_shape, row_shape, jax.ShapeDtypeStruct((1, d), F32)],
        [pltpu.VMEM((mp, 4 * n, d), BF16), pltpu.VMEM((mp, 4, chunk, n), BF16)] + scratch * 2
        + [pltpu.SemaphoreType.DMA((3 + (mp - 2) * parts,))],
    )(hist_len, meta, flat_states, normed, mcot, gain, all0, all1, qkv_rows, wo_rows, wt1, *rest)

    summed = kept[0]
    for part in arrived:
        summed = summed + part.astype(F32)
    gain_sum = gain_part
    for r in range(1, parts):
        gain_sum = gain_sum + hop_dp(gain_part, r)
    gain_piece = lax.dynamic_slice_in_dim(gain_sum.reshape(d), i_hi * (d // parts), d // parts, 0)
    if low > 1:
        groups = [[hi * low + lo for lo in range(low)] for hi in range(parts)]
        summed = lax.psum_scatter(summed, "dp", scatter_dimension=0, axis_index_groups=groups, tiled=True)
        gain_piece = lax.psum_scatter(gain_piece, "dp", scatter_dimension=0, axis_index_groups=groups, tiled=True)
    across = summed.T
    grad_qkv = jnp.transpose(across[: 3 * n].reshape(3, heads, width, -1), (3, 0, 1, 2))
    grad_output = across[3 * n :].reshape(heads, width, -1)
    return (attended.reshape(batch, seq, d), grad_states.reshape(batch, seq, d), grad_qkv, grad_output, gain_piece)


def solution(mesh):
    placed = (
        P("dp", None, None),
        P("dp"),
        P(),
        P(None, None, "mp", None),
        P("mp", None, None),
        P("dp", None, None),
    )
    return jax.shard_map(
        functools.partial(body, mesh.shape["dp"], mesh.shape["mp"]),
        mesh=mesh,
        in_specs=placed,
        out_specs=(
            P("dp", None, None),
            P("dp", None, None),
            P("dp", None, "mp", None),
            P("mp", None, "dp"),
            P("dp"),
        ),
        check_vma=False,
    )
```

profile of v0, /device:TPU:0, one launch (start us, length us, event | category | flops | bytes accessed | tf_op | source)
XLA Modules:
  0.0 114.8 jit_solution(6101866577278094960)
XLA Ops:
  1.6 3.1 %collective-permute-start = (bf16[96,768]{1,0:T(8,128)(2,1)S(1)}, bf16[96,768]{1,0:T(8,128)(2,1)S(1)}, u32[]{:S(2)}, u32[]{:S(2)}) collective-permute-start(bf16[96,768]{1,0:T(8,128)(2,1)S(1)} %fusion.7), channel_id=1, source_target_pairs={{0,1},{1,0},{2,3},{3,2},{4,5},{5,4},{6,7},{7,6},{8,9},{9,8},{10,11... | collective-permute-start | bytes 442376 | tf_op jit(solution)/shard_map/ppermute | solution.py:208
  4.7 2.6 %collective-permute-start.8 = (bf16[96,768]{1,0:T(8,128)(2,1)S(1)}, bf16[96,768]{1,0:T(8,128)(2,1)S(1)}, u32[]{:S(2)}, u32[]{:S(2)}) collective-permute-start(bf16[96,768]{1,0:T(8,128)(2,1)S(1)} %fusion.7), channel_id=1, source_target_pairs={{0,2},{1,3},{2,0},{3,1},{4,6},{5,7},{6,4},{7,5},{8,10},{9,11},{10,... | collective-permute-start | bytes 442376 | tf_op jit(solution)/shard_map/ppermute | solution.py:208
  8.0 2.6 %collective-permute-done.refs_0_ = bf16[96,768]{1,0:T(8,128)(2,1)S(1)} collective-permute-done((bf16[96,768]{1,0:T(8,128)(2,1)S(1)}, bf16[96,768]{1,0:T(8,128)(2,1)S(1)}, u32[]{:S(2)}, u32[]{:S(2)}) %collective-permute-start) | collective-permute-done | bytes 147488 | tf_op jit(solution)/shard_map/ppermute | solution.py:208
  10.6 1.7 %collective-permute-start.2 = (bf16[96,768]{1,0:T(8,128)(2,1)S(1)}, bf16[96,768]{1,0:T(8,128)(2,1)S(1)}, u32[]{:S(2)}, u32[]{:S(2)}) collective-permute-start(bf16[96,768]{1,0:T(8,128)(2,1)S(1)} %collective-permute-done.refs_0_), channel_id=1, source_target_pairs={{0,8},{4,12},{8,0},{12,4},{16,24},{20,28},{24,16},{28,20},{1,9},{5... | collective-permute-start | bytes 442376 | tf_op jit(solution)/shard_map/ppermute | solution.py:205
  14.5 1.5 %copy-done.10 = bf16[16,80,768]{2,1,0:T(8,128)(2,1)S(1)} copy-done((bf16[16,80,768]{2,1,0:T(8,128)(2,1)S(1)}, bf16[16,80,768]{2,1,0:T(8,128)(2,1)}, u32[]{:S(2)}) %copy-start.10) | copy-done | bytes 1966104
  16.0 1.5 %copy-done.11 = bf16[16,80,768]{2,1,0:T(8,128)(2,1)S(1)} copy-done((bf16[16,80,768]{2,1,0:T(8,128)(2,1)S(1)}, bf16[16,80,768]{2,1,0:T(8,128)(2,1)}, u32[]{:S(2)}) %copy-start.11) | copy-done | bytes 1966104
  18.2 9.0 %shard_map.101 = (bf16[1280,768]{1,0:T(8,128)(2,1)S(1)}, bf16[1280,768]{1,0:T(8,128)(2,1)S(1)}, bf16[4,1280,192]{2,1,0:T(8,128)(2,1)S(1)}) custom-call(s32[16]{0:T(128)S(1)} %copy-done.13, bf16[1280,768]{1,0:T(8,128)(2,1)S(1)} %bitcast.47, bf16[1280,768]{1,0:T(8,128)(2,1)S(1)} %bitcast.46, f32[1,768]{1,0:T(1,128)S(1)} %reshape.49.gain_ref, ...), custom_call_target="tpu_custom_call" | custom-call | flops 4529848320 | bytes 7864320 | tf_op jit(solution)/shard_map/pallas_call | solution.py:255
  28.5 1.3 %copy-done.4 = bf16[1280,768]{1,0:T(8,128)(2,1)} copy-done((bf16[1280,768]{1,0:T(8,128)(2,1)}, bf16[1280,768]{1,0:T(8,128)(2,1)S(1)}, u32[]{:S(2)}) %copy-start.4) | copy-done | bytes 1966104
  29.8 1.5 %collective-permute-start.4 = (bf16[96,768]{1,0:T(8,128)(2,1)S(1)}, bf16[96,768]{1,0:T(8,128)(2,1)S(1)}, u32[]{:S(2)}, u32[]{:S(2)}) collective-permute-start(bf16[96,768]{1,0:T(8,128)(2,1)S(1)} %collective-permute-done.refs_0_), channel_id=1, source_target_pairs={{0,16},{4,20},{8,24},{12,28},{16,0},{20,4},{24,8},{28,12},{1,17},{... | collective-permute-start | bytes 442376 | tf_op jit(solution)/shard_map/ppermute | solution.py:205
  32.2 1.8 %collective-permute-start.11 = (bf16[2,96,768]{2,1,0:T(8,128)(2,1)S(1)}, bf16[2,96,768]{2,1,0:T(8,128)(2,1)S(1)}, u32[]{:S(2)}, u32[]{:S(2)}) collective-permute-start(bf16[2,96,768]{2,1,0:T(8,128)(2,1)S(1)} %pad_maximum_fusion.refs_0_), channel_id=1, source_target_pairs={{0,8},{4,12},{8,0},{12,4},{16,24},{20,28},{24,16},{28,20},{1,9},{5... | collective-permute-start | bytes 884744 | tf_op jit(solution)/shard_map/ppermute | solution.py:205
  34.9 1.7 %collective-permute-start.13 = (bf16[2,96,768]{2,1,0:T(8,128)(2,1)S(1)}, bf16[2,96,768]{2,1,0:T(8,128)(2,1)S(1)}, u32[]{:S(2)}, u32[]{:S(2)}) collective-permute-start(bf16[2,96,768]{2,1,0:T(8,128)(2,1)S(1)} %pad_maximum_fusion.refs_0_), channel_id=1, source_target_pairs={{0,16},{4,20},{8,24},{12,28},{16,0},{20,4},{24,8},{28,12},{1,17},{... | collective-permute-start | bytes 884744 | tf_op jit(solution)/shard_map/ppermute | solution.py:205
  36.7 2.0 %collective-permute-done.6.refs_6_ = bf16[96,768]{1,0:T(8,128)(2,1)S(1)} collective-permute-done((bf16[96,768]{1,0:T(8,128)(2,1)S(1)}, bf16[96,768]{1,0:T(8,128)(2,1)S(1)}, u32[]{:S(2)}, u32[]{:S(2)}) %collective-permute-start.6) | collective-permute-done | bytes 147488 | tf_op jit(solution)/shard_map/ppermute | solution.py:205
  38.7 1.5 %copy-done.2 = bf16[1280,768]{1,0:T(8,128)(2,1)S(1)} copy-done((bf16[1280,768]{1,0:T(8,128)(2,1)S(1)}, bf16[1280,768]{1,0:T(8,128)(2,1)}, u32[]{:S(2)}) %copy-start.2) | copy-done | bytes 1966104
  40.2 1.5 %copy-done.5 = bf16[1280,768]{1,0:T(8,128)(2,1)S(1)} copy-done((bf16[1280,768]{1,0:T(8,128)(2,1)S(1)}, bf16[1280,768]{1,0:T(8,128)(2,1)}, u32[]{:S(2)}) %copy-start.5) | copy-done | bytes 1966104
  41.7 3.8 %shard_map.104 = (f32[96,768]{1,0:T(8,128)S(1)}, f32[96,768]{1,0:T(8,128)S(1)}, f32[96,768]{1,0:T(8,128)S(1)}, f32[96,768]{1,0:T(8,128)S(1)}, bf16[4,96,768]{2,1,0:T(8,128)(2,1)S(1)}) custom-call(s32[2]{0:T(128)S(1)} %pad_add_fusion.meta_ref, bf16[1280,768]{1,0:T(8,128)(2,1)S(1)} %copy-done.2, bf16[1280,768]{1,0:T(8,128)(2,1)S(1)} %copy-done.5, ...), custom_call_target="tpu_custom_call" | custom-call | flops 1509949440 | bytes 7864320 | tf_op jit(solution)/shard_map/pallas_call | solution.py:263
  46.3 1.8 %collective-permute-done.7.refs_7_ = bf16[96,768]{1,0:T(8,128)(2,1)S(1)} collective-permute-done((bf16[96,768]{1,0:T(8,128)(2,1)S(1)}, bf16[96,768]{1,0:T(8,128)(2,1)S(1)}, u32[]{:S(2)}, u32[]{:S(2)}) %collective-permute-start.7) | collective-permute-done | bytes 147488 | tf_op jit(solution)/shard_map/ppermute | solution.py:205
  48.6 1.6 %collective-permute-done.13.refs_4_ = bf16[2,96,768]{2,1,0:T(8,128)(2,1)S(1)} collective-permute-done((bf16[2,96,768]{2,1,0:T(8,128)(2,1)S(1)}, bf16[2,96,768]{2,1,0:T(8,128)(2,1)S(1)}, u32[]{:S(2)}, u32[]{:S(2)}) %collective-permute-start.13) | collective-permute-done | bytes 294944 | tf_op jit(solution)/shard_map/ppermute | solution.py:205
  50.6 10.4 %shard_map.102 = (bf16[4,1280,192]{2,1,0:T(8,128)(2,1)S(1)}, bf16[768,768]{1,0:T(8,128)(2,1)S(1)}) custom-call(s32[16]{0:T(128)S(1)} %copy-done.14, s32[2]{0:T(128)S(1)} %pad_add_fusion.meta_ref, bf16[1280,768]{1,0:T(8,128)(2,1)S(1)} %copy-done.3, bf16[1280,768]{1,0:T(8,128)(2,1)S(1)} %copy-done.5, bf16[96,768]{1,0:T(8,128)(2,1)S(1)} %collective-permute-done.refs_0_, ...), custom_call_target="tpu_custom_call" | custom-call | flops 4529848320 | bytes 7864320 | tf_op jit(solution)/shard_map/pallas_call | solution.py:274
  61.0 1.5 %copy-done.15 = bf16[4,1280,192]{2,1,0:T(8,128)(2,1)} copy-done((bf16[4,1280,192]{2,1,0:T(8,128)(2,1)}, bf16[4,1280,192]{2,1,0:T(8,128)(2,1)S(1)}, u32[]{:S(2)}) %copy-start.15) | copy-done | bytes 1966104
  63.3 1.3 %collective-permute-start.19 = (bf16[96,768]{1,0:T(8,128)(2,1)S(1)}, bf16[96,768]{1,0:T(8,128)(2,1)S(1)}, u32[]{:S(2)}, u32[]{:S(2)}) collective-permute-start(bf16[96,768]{1,0:T(8,128)(2,1)S(1)} %get-tuple-element.38), channel_id=1, source_target_pairs={{0,16},{4,20},{8,24},{12,28},{16,0},{20,4},{24,8},{28,12},{1,17},{... | collective-permute-start | bytes 442376 | tf_op jit(solution)/shard_map/ppermute | solution.py:205
  64.6 1.6 %collective-permute-start.20 = (bf16[96,768]{1,0:T(8,128)(2,1)S(1)}, bf16[96,768]{1,0:T(8,128)(2,1)S(1)}, u32[]{:S(2)}, u32[]{:S(2)}) collective-permute-start(bf16[96,768]{1,0:T(8,128)(2,1)S(1)} %get-tuple-element.37), channel_id=1, source_target_pairs={{0,24},{4,28},{8,16},{12,20},{16,8},{20,12},{24,0},{28,4},{1,25},{... | collective-permute-start | bytes 442376 | tf_op jit(solution)/shard_map/ppermute | solution.py:205
  66.2 39.1 %shard_map.103 = (bf16[1280,768]{1,0:T(8,128)(2,1)}, bf16[1280,768]{1,0:T(8,128)(2,1)}, f32[1,768]{1,0:T(1,128)S(1)}) custom-call(s32[16]{0:T(128)S(1)} %copy-done.14, s32[2]{0:T(128)S(1)} %pad_add_fusion.meta_ref, bf16[1280,768]{1,0:T(8,128)(2,1)S(1)} %bitcast.48, bf16[1280,768]{1,0:T(8,128)(2,1)S(1)} %copy-done.3, bf16[1280,768]{1,0:T(8,128)(2,1)} %copy-done.4, ...), custom_call_target="tpu_custom_call" | custom-call | flops 15099494400 | bytes 7864320 | tf_op jit(solution)/shard_map/pallas_call | solution.py:281
  109.0 1.4 %collective-permute-start.26 = (f32[1,768]{1,0:T(1,128)S(1)}, f32[1,768]{1,0:T(1,128)S(1)}, u32[]{:S(2)}, u32[]{:S(2)}) collective-permute-start(f32[1,768]{1,0:T(1,128)S(1)} %get-tuple-element.30), channel_id=1, source_target_pairs={{0,24},{4,28},{8,16},{12,20},{16,8},{20,12},{24,0},{28,4},{1,25},{... | collective-permute-start | bytes 9224 | tf_op jit(solution)/shard_map/ppermute | solution.py:205
  110.3 1.3 %collective-permute-start.27 = (f32[1,768]{1,0:T(1,128)S(1)}, f32[1,768]{1,0:T(1,128)S(1)}, u32[]{:S(2)}, u32[]{:S(2)}) collective-permute-start(f32[1,768]{1,0:T(1,128)S(1)} %get-tuple-element.30), channel_id=1, source_target_pairs={{0,28},{4,24},{8,20},{12,16},{16,12},{20,8},{24,4},{28,0},{1,29},{... | collective-permute-start | bytes 9224 | tf_op jit(solution)/shard_map/ppermute | solution.py:205
  (80 shorter events, 16.9 us)
Async XLA Ops:
  1.6 9.0 %collective-permute-start = (bf16[96,768]{1,0:T(8,128)(2,1)S(1)}, bf16[96,768]{1,0:T(8,128)(2,1)S(1)}, u32[]{:S(2)}, u32[]{:S(2)}) collective-permute-start(bf16[96,768]{1,0:T(8,128)(2,1)S(1)} %fusion.7), channel_id=1, source_target_pairs={{0,1},{1,0},{2,3},{3,2},{4,5},{5,4},{6,7},{7,6},{8,9},{9,8},{10,11... | collective-permute-start | bytes 442376 | tf_op jit(solution)/shard_map/ppermute | solution.py:208
  4.7 26.8 %collective-permute-start.8 = (bf16[96,768]{1,0:T(8,128)(2,1)S(1)}, bf16[96,768]{1,0:T(8,128)(2,1)S(1)}, u32[]{:S(2)}, u32[]{:S(2)}) collective-permute-start(bf16[96,768]{1,0:T(8,128)(2,1)S(1)} %fusion.7), channel_id=1, source_target_pairs={{0,2},{1,3},{2,0},{3,1},{4,6},{5,7},{6,4},{7,5},{8,10},{9,11},{10,... | collective-permute-start | bytes 442376 | tf_op jit(solution)/shard_map/ppermute | solution.py:208
  7.3 24.8 %collective-permute-start.9 = (bf16[96,768]{1,0:T(8,128)(2,1)S(1)}, bf16[96,768]{1,0:T(8,128)(2,1)S(1)}, u32[]{:S(2)}, u32[]{:S(2)}) collective-permute-start(bf16[96,768]{1,0:T(8,128)(2,1)S(1)} %fusion.7), channel_id=1, source_target_pairs={{0,3},{1,2},{2,1},{3,0},{4,7},{5,6},{6,5},{7,4},{8,11},{9,10},{10,... | collective-permute-start | bytes 442376 | tf_op jit(solution)/shard_map/ppermute | solution.py:208
  10.6 21.0 %collective-permute-start.2 = (bf16[96,768]{1,0:T(8,128)(2,1)S(1)}, bf16[96,768]{1,0:T(8,128)(2,1)S(1)}, u32[]{:S(2)}, u32[]{:S(2)}) collective-permute-start(bf16[96,768]{1,0:T(8,128)(2,1)S(1)} %collective-permute-done.refs_0_), channel_id=1, source_target_pairs={{0,8},{4,12},{8,0},{12,4},{16,24},{20,28},{24,16},{28,20},{1,9},{5... | collective-permute-start | bytes 442376 | tf_op jit(solution)/shard_map/ppermute | solution.py:205
  29.8 5.1 %collective-permute-start.4 = (bf16[96,768]{1,0:T(8,128)(2,1)S(1)}, bf16[96,768]{1,0:T(8,128)(2,1)S(1)}, u32[]{:S(2)}, u32[]{:S(2)}) collective-permute-start(bf16[96,768]{1,0:T(8,128)(2,1)S(1)} %collective-permute-done.refs_0_), channel_id=1, source_target_pairs={{0,16},{4,20},{8,24},{12,28},{16,0},{20,4},{24,8},{28,12},{1,17},{... | collective-permute-start | bytes 442376 | tf_op jit(solution)/shard_map/ppermute | solution.py:205
  31.3 7.3 %collective-permute-start.6 = (bf16[96,768]{1,0:T(8,128)(2,1)S(1)}, bf16[96,768]{1,0:T(8,128)(2,1)S(1)}, u32[]{:S(2)}, u32[]{:S(2)}) collective-permute-start(bf16[96,768]{1,0:T(8,128)(2,1)S(1)} %collective-permute-done.refs_0_), channel_id=1, source_target_pairs={{0,24},{4,28},{8,16},{12,20},{16,8},{20,12},{24,0},{28,4},{1,25},{... | collective-permute-start | bytes 442376 | tf_op jit(solution)/shard_map/ppermute | solution.py:205
  31.6 7.1 %collective-permute-start.1 = (bf16[96,768]{1,0:T(8,128)(2,1)S(1)}, bf16[96,768]{1,0:T(8,128)(2,1)S(1)}, u32[]{:S(2)}, u32[]{:S(2)}) collective-permute-start(bf16[96,768]{1,0:T(8,128)(2,1)S(1)} %collective-permute-done.refs_0_), channel_id=1, source_target_pairs={{0,4},{4,0},{8,12},{12,8},{16,20},{20,16},{24,28},{28,24},{1,5},{5... | collective-permute-start | bytes 442376 | tf_op jit(solution)/shard_map/ppermute | solution.py:205
  31.6 14.0 %collective-permute-start.3 = (bf16[96,768]{1,0:T(8,128)(2,1)S(1)}, bf16[96,768]{1,0:T(8,128)(2,1)S(1)}, u32[]{:S(2)}, u32[]{:S(2)}) collective-permute-start(bf16[96,768]{1,0:T(8,128)(2,1)S(1)} %collective-permute-done.2.refs_2_), channel_id=1, source_target_pairs={{0,4},{4,0},{8,12},{12,8},{16,20},{20,16},{24,28},{28,24},{1,5},{5... | collective-permute-start | bytes 442376 | tf_op jit(solution)/shard_map/ppermute | solution.py:205
  32.2 16.2 %collective-permute-start.11 = (bf16[2,96,768]{2,1,0:T(8,128)(2,1)S(1)}, bf16[2,96,768]{2,1,0:T(8,128)(2,1)S(1)}, u32[]{:S(2)}, u32[]{:S(2)}) collective-permute-start(bf16[2,96,768]{2,1,0:T(8,128)(2,1)S(1)} %pad_maximum_fusion.refs_0_), channel_id=1, source_target_pairs={{0,8},{4,12},{8,0},{12,4},{16,24},{20,28},{24,16},{28,20},{1,9},{5... | collective-permute-start | bytes 884744 | tf_op jit(solution)/shard_map/ppermute | solution.py:205
  34.9 15.2 %collective-permute-start.13 = (bf16[2,96,768]{2,1,0:T(8,128)(2,1)S(1)}, bf16[2,96,768]{2,1,0:T(8,128)(2,1)S(1)}, u32[]{:S(2)}, u32[]{:S(2)}) collective-permute-start(bf16[2,96,768]{2,1,0:T(8,128)(2,1)S(1)} %pad_maximum_fusion.refs_0_), channel_id=1, source_target_pairs={{0,16},{4,20},{8,24},{12,28},{16,0},{20,4},{24,8},{28,12},{1,17},{... | collective-permute-start | bytes 884744 | tf_op jit(solution)/shard_map/ppermute | solution.py:205
  38.6 11.5 %collective-permute-start.15 = (bf16[2,96,768]{2,1,0:T(8,128)(2,1)S(1)}, bf16[2,96,768]{2,1,0:T(8,128)(2,1)S(1)}, u32[]{:S(2)}, u32[]{:S(2)}) collective-permute-start(bf16[2,96,768]{2,1,0:T(8,128)(2,1)S(1)} %pad_maximum_fusion.refs_0_), channel_id=1, source_target_pairs={{0,24},{4,28},{8,16},{12,20},{16,8},{20,12},{24,0},{28,4},{1,25},{... | collective-permute-start | bytes 884744 | tf_op jit(solution)/shard_map/ppermute | solution.py:205
  38.6 7.6 %collective-permute-start.5 = (bf16[96,768]{1,0:T(8,128)(2,1)S(1)}, bf16[96,768]{1,0:T(8,128)(2,1)S(1)}, u32[]{:S(2)}, u32[]{:S(2)}) collective-permute-start(bf16[96,768]{1,0:T(8,128)(2,1)S(1)} %collective-permute-done.4.refs_4_), channel_id=1, source_target_pairs={{0,4},{4,0},{8,12},{12,8},{16,20},{20,16},{24,28},{28,24},{1,5},{5... | collective-permute-start | bytes 442376 | tf_op jit(solution)/shard_map/ppermute | solution.py:205
  45.6 16.9 %collective-permute-start.17 = (bf16[4,96,768]{2,1,0:T(8,128)(2,1)S(1)}, bf16[4,96,768]{2,1,0:T(8,128)(2,1)S(1)}, u32[]{:S(2)}, u32[]{:S(2)}) collective-permute-start(bf16[4,96,768]{2,1,0:T(8,128)(2,1)S(1)} %get-tuple-element.26), channel_id=1, source_target_pairs={{0,4},{4,0},{8,12},{12,8},{16,20},{20,16},{24,28},{28,24},{1,5},{5... | collective-permute-start | bytes 1769480 | tf_op jit(solution)/shard_map/ppermute | solution.py:205
  48.0 15.3 %collective-permute-start.10 = (bf16[2,96,768]{2,1,0:T(8,128)(2,1)S(1)}, bf16[2,96,768]{2,1,0:T(8,128)(2,1)S(1)}, u32[]{:S(2)}, u32[]{:S(2)}) collective-permute-start(bf16[2,96,768]{2,1,0:T(8,128)(2,1)S(1)} %pad_maximum_fusion.refs_0_), channel_id=1, source_target_pairs={{0,4},{4,0},{8,12},{12,8},{16,20},{20,16},{24,28},{28,24},{1,5},{5... | collective-permute-start | bytes 884744 | tf_op jit(solution)/shard_map/ppermute | solution.py:205
  48.4 16.2 %collective-permute-start.12 = (bf16[2,96,768]{2,1,0:T(8,128)(2,1)S(1)}, bf16[2,96,768]{2,1,0:T(8,128)(2,1)S(1)}, u32[]{:S(2)}, u32[]{:S(2)}) collective-permute-start(bf16[2,96,768]{2,1,0:T(8,128)(2,1)S(1)} %collective-permute-done.11.refs_2_), channel_id=1, source_target_pairs={{0,4},{4,0},{8,12},{12,8},{16,20},{20,16},{24,28},{28,24},{1,5},{5... | collective-permute-start | bytes 884744 | tf_op jit(solution)/shard_map/ppermute | solution.py:205
  50.1 16.1 %collective-permute-start.14 = (bf16[2,96,768]{2,1,0:T(8,128)(2,1)S(1)}, bf16[2,96,768]{2,1,0:T(8,128)(2,1)S(1)}, u32[]{:S(2)}, u32[]{:S(2)}) collective-permute-start(bf16[2,96,768]{2,1,0:T(8,128)(2,1)S(1)} %collective-permute-done.13.refs_4_), channel_id=1, source_target_pairs={{0,4},{4,0},{8,12},{12,8},{16,20},{20,16},{24,28},{28,24},{1,5},{5... | collective-permute-start | bytes 884744 | tf_op jit(solution)/shard_map/ppermute | solution.py:205
  50.1 16.1 %collective-permute-start.16 = (bf16[2,96,768]{2,1,0:T(8,128)(2,1)S(1)}, bf16[2,96,768]{2,1,0:T(8,128)(2,1)S(1)}, u32[]{:S(2)}, u32[]{:S(2)}) collective-permute-start(bf16[2,96,768]{2,1,0:T(8,128)(2,1)S(1)} %collective-permute-done.15.refs_6_), channel_id=1, source_target_pairs={{0,4},{4,0},{8,12},{12,8},{16,20},{20,16},{24,28},{28,24},{1,5},{5... | collective-permute-start | bytes 884744 | tf_op jit(solution)/shard_map/ppermute | solution.py:205
  62.6 43.5 %collective-permute-start.18 = (bf16[96,768]{1,0:T(8,128)(2,1)S(1)}, bf16[96,768]{1,0:T(8,128)(2,1)S(1)}, u32[]{:S(2)}, u32[]{:S(2)}) collective-permute-start(bf16[96,768]{1,0:T(8,128)(2,1)S(1)} %get-tuple-element.36), channel_id=1, source_target_pairs={{0,8},{4,12},{8,0},{12,4},{16,24},{20,28},{24,16},{28,20},{1,9},{5... | collective-permute-start | bytes 442376 | tf_op jit(solution)/shard_map/ppermute | solution.py:205
  63.3 43.9 %collective-permute-start.19 = (bf16[96,768]{1,0:T(8,128)(2,1)S(1)}, bf16[96,768]{1,0:T(8,128)(2,1)S(1)}, u32[]{:S(2)}, u32[]{:S(2)}) collective-permute-start(bf16[96,768]{1,0:T(8,128)(2,1)S(1)} %get-tuple-element.38), channel_id=1, source_target_pairs={{0,16},{4,20},{8,24},{12,28},{16,0},{20,4},{24,8},{28,12},{1,17},{... | collective-permute-start | bytes 442376 | tf_op jit(solution)/shard_map/ppermute | solution.py:205
  64.6 43.7 %collective-permute-start.20 = (bf16[96,768]{1,0:T(8,128)(2,1)S(1)}, bf16[96,768]{1,0:T(8,128)(2,1)S(1)}, u32[]{:S(2)}, u32[]{:S(2)}) collective-permute-start(bf16[96,768]{1,0:T(8,128)(2,1)S(1)} %get-tuple-element.37), channel_id=1, source_target_pairs={{0,24},{4,28},{8,16},{12,20},{16,8},{20,12},{24,0},{28,4},{1,25},{... | collective-permute-start | bytes 442376 | tf_op jit(solution)/shard_map/ppermute | solution.py:205
  105.4 4.9 %collective-permute-start.22 = (f32[1,768]{1,0:T(1,128)S(1)}, f32[1,768]{1,0:T(1,128)S(1)}, u32[]{:S(2)}, u32[]{:S(2)}) collective-permute-start(f32[1,768]{1,0:T(1,128)S(1)} %get-tuple-element.30), channel_id=1, source_target_pairs={{0,8},{4,12},{8,0},{12,4},{16,24},{20,28},{24,16},{28,20},{1,9},{5... | collective-permute-start | bytes 9224 | tf_op jit(solution)/shard_map/ppermute | solution.py:205
  106.1 7.4 %collective-permute-start.23 = (f32[1,768]{1,0:T(1,128)S(1)}, f32[1,768]{1,0:T(1,128)S(1)}, u32[]{:S(2)}, u32[]{:S(2)}) collective-permute-start(f32[1,768]{1,0:T(1,128)S(1)} %get-tuple-element.30), channel_id=1, source_target_pairs={{0,12},{4,8},{8,4},{12,0},{16,28},{20,24},{24,20},{28,16},{1,13},{... | collective-permute-start | bytes 9224 | tf_op jit(solution)/shard_map/ppermute | solution.py:205
  107.2 6.2 %collective-permute-start.24 = (f32[1,768]{1,0:T(1,128)S(1)}, f32[1,768]{1,0:T(1,128)S(1)}, u32[]{:S(2)}, u32[]{:S(2)}) collective-permute-start(f32[1,768]{1,0:T(1,128)S(1)} %get-tuple-element.30), channel_id=1, source_target_pairs={{0,16},{4,20},{8,24},{12,28},{16,0},{20,4},{24,8},{28,12},{1,17},{... | collective-permute-start | bytes 9224 | tf_op jit(solution)/shard_map/ppermute | solution.py:205
  108.4 5.1 %collective-permute-start.25 = (f32[1,768]{1,0:T(1,128)S(1)}, f32[1,768]{1,0:T(1,128)S(1)}, u32[]{:S(2)}, u32[]{:S(2)}) collective-permute-start(f32[1,768]{1,0:T(1,128)S(1)} %get-tuple-element.30), channel_id=1, source_target_pairs={{0,20},{4,16},{8,28},{12,24},{16,4},{20,0},{24,12},{28,8},{1,21},{... | collective-permute-start | bytes 9224 | tf_op jit(solution)/shard_map/ppermute | solution.py:205
  (20 other events, 122.4 us)
where the time goes:
time: 115 us
  Pallas kernels  62.3 us (54%)
  starting transfers between devices  24.8 us (22%)
  local copies, waits for them, and re-layouts  15.4 us (13%)
  waiting for transfers between devices  9.65 us (8%)
  other arithmetic  1.87 us (2%)
    pallas_call x1, Pallas kernels, body(): call(functools.partial(final_kernel, seq, heads, width, parts, mp), 10 *...  39.1 us
    ppermute x25, starting transfers between devices, hop_dp(): return lax.ppermute(x, 'dp', [(i, i ^ r * low) for i in range(dp)])  19.1 us
    unnamed x32, local copies, waits for them, and re-layouts  13 us
    pallas_call x1, Pallas kernels, body(): call(functools.partial(far_kernel, seq, heads, width, parts), 3 * flops_i...  10.4 us
    pallas_call x1, Pallas kernels, body(): call(functools.partial(own_kernel, seq, heads, width), 3 * flops_in, 24,...  8.99 us
    ppermute x25, waiting for transfers between devices, hop_dp(): return lax.ppermute(x, 'dp', [(i, i ^ r * low) for i in range(dp)])  7.03 us
    ppermute x3, starting transfers between devices, hop_mp(): return lax.ppermute(x, 'mp', [(i, i ^ k) for i in range(mp)])  5.71 us
    pallas_call x1, Pallas kernels, body(): call(functools.partial(weight_grad_kernel, parts, n), flops_in, 32, 1, 2,...  3.82 us
  transfers between devices with their start and end apart: 28, of which 6 were waited for; matrix products, arithmetic and copies ran while one was open for 2% of the time, Pallas kernels for 54%

commit v1 on v0

--- a/solution.py
+++ b/solution.py
@@ -26,24 +26,16 @@
     return lax.dot_general(a, b, (((0,), (0,)), ((), ())), preferred_element_type=F32)
 
 
-def attention(q, k, v, g, valid, heads, width):
-    seq = q.shape[0]
+def attention(refs, out_ref, valid, heads, width):
+    q_s, k_s, v_s, g_s = refs
+    count = len(valid)
+    seq = q_s.shape[0] // count
     lane_head = lax.broadcasted_iota(jnp.int32, (1, heads * width), 1) // width
     masks = [(lane_head == h).astype(BF16) for h in range(heads)]
-    q_blocks = jnp.concatenate([q * m for m in masks], axis=0)
-    g_blocks = jnp.concatenate([g * m for m in masks], axis=0)
-    scores = dot_nt(k, q_blocks)
-    row = lax.broadcasted_iota(jnp.int32, scores.shape, 0)
-    scores = jnp.where(row < valid, scores, -1e30)
-    top = jnp.max(scores, axis=0, keepdims=True)
-    exp_scores = jnp.exp(scores - top)
-    prob = exp_scores * (1.0 / jnp.sum(exp_scores, axis=0, keepdims=True))
-    prob_bf = prob.astype(BF16)
-    grad_prob = dot_nt(v, g_blocks)
-    delta = jnp.sum(prob * grad_prob, axis=0, keepdims=True)
-    grad_scores = (prob * (grad_prob - delta)).astype(BF16)
-    grad_v = dot_nn(prob_bf, g_blocks)
-    grad_k = dot_nn(grad_scores, q_blocks)
+    rows = [slice(b * seq, (b + 1) * seq) for b in range(count)]
+
+    def blocks(x):
+        return jnp.concatenate([x * m for m in masks], axis=0)
 
     def diagonal(full):
         out = full[:seq]
@@ -51,9 +43,22 @@
             out = jnp.where(lane_head == h, full[h * seq : (h + 1) * seq], out)
         return out
 
-    context = diagonal(dot_tn(prob_bf, v))
-    grad_q = diagonal(dot_tn(grad_scores, k))
-    return grad_q, grad_k, grad_v, context
+    scores = [dot_nt(k_s[r], blocks(q_s[r])) for r in rows]
+    grad_prob = [dot_nt(v_s[r], blocks(g_s[r])) for r in rows]
+    probs, grad_scores = [], []
+    for score, grad, length in zip(scores, grad_prob, valid):
+        row = lax.broadcasted_iota(jnp.int32, score.shape, 0)
+        score = jnp.where(row < length, score, -1e30)
+        exp_score = jnp.exp(score - jnp.max(score, axis=0, keepdims=True))
+        prob = exp_score * (1.0 / jnp.sum(exp_score, axis=0, keepdims=True))
+        probs.append(prob.astype(BF16))
+        delta = jnp.sum(prob * grad, axis=0, keepdims=True)
+        grad_scores.append((prob * (grad - delta)).astype(BF16))
+    for r, prob, grad_score in zip(rows, probs, grad_scores):
+        out_ref[2, r] = dot_nn(prob, blocks(g_s[r])).astype(BF16)
+        out_ref[1, r] = dot_nn(grad_score, blocks(q_s[r])).astype(BF16)
+        out_ref[3, r] = diagonal(dot_tn(prob, v_s[r])).astype(BF16)
+        out_ref[0, r] = diagonal(dot_tn(grad_score, k_s[r])).astype(BF16)
 
 
 def keep_rows(len_ref, first, count, seq):
@@ -69,12 +74,7 @@
     k_s[...] = dot_nt(normed, w_k).astype(BF16)
     v_s[...] = dot_nt(normed, w_v).astype(BF16)
     g_s[...] = dot_nt(mcot, w_o).astype(BF16)
-    for b in range(count):
-        rows = slice(b * seq, (b + 1) * seq)
-        valid = LEVELS * len_ref[chunk * count + b]
-        parts = attention(q_s[rows], k_s[rows], v_s[rows], g_s[rows], valid, heads, width)
-        for n, part in enumerate(parts):
-            out_ref[n, rows] = part.astype(BF16)
+    attention(scratch, out_ref, [LEVELS * len_ref[chunk * count + b] for b in range(count)], heads, width)
 
 
 def own_kernel(seq, heads, width, len_ref, states_ref, cot_ref, gain_ref, qkv_ref, wo_ref,
@@ -92,18 +92,17 @@
                out_ref.at[:], scratch, seq, heads, width)
 
 
-def far_kernel(seq, heads, width, parts, len_ref, meta_ref, normed_ref, mcot_ref, *refs):
-    blocks = refs[:parts]
-    out_ref, wt_ref, q_s, k_s, v_s, g_s, sems = refs[parts:]
+def far_kernel(seq, heads, width, len_ref, meta_ref, normed_ref, mcot_ref, *refs):
+    blocks = refs[:4]
+    out_ref, wt_ref, q_s, k_s, v_s, g_s, sems = refs[4:]
     n = heads * width
-    size = 4 * n // parts
 
     @pl.when(pl.program_id(0) == 0)
     def _():
         copies = []
-        for r in range(parts):
-            place = pl.multiple_of((meta_ref[1] ^ r) * size, 8)
-            copies.append(pltpu.make_async_copy(blocks[r], wt_ref.at[pl.ds(place, size)], sems.at[r]))
+        for r in range(4):
+            place = pl.multiple_of(((meta_ref[1] % 4) ^ r) * n, 8)
+            copies.append(pltpu.make_async_copy(blocks[r], wt_ref.at[pl.ds(place, n)], sems.at[r]))
         for copy in copies:
             copy.start()
         for copy in copies:
@@ -171,17 +170,25 @@
         w = [wt_s[own ^ k, i * n : (i + 1) * n] for i in range(4)]
         shard_body(len_ref, normed, mcot, w[0], w[1], w[2], w[3],
                    all_s.at[own ^ k], scratch[4 * (k % 2) : 4 * (k % 2) + 4], seq, heads, width)
-    total = None
-    grad = None
-    for s in range(shards):
-        piece = dot_nn(all_s[s, 3], wt_s[s, 3 * n :])
-        total = piece if total is None else total + piece
+
+    def chain(kinds, rows, columns):
+        out = None
+        for s in range(shards):
+            for i in kinds:
+                piece = dot_nn(all_s[s, i, rows], wt_s[s, i * n : (i + 1) * n, columns])
+                out = piece if out is None else out + piece
+        return out
+
+    def project(kinds):
+        count, d = states_ref.shape
+        cut, half = d - 256, count // 2
+        last = [chain(kinds, slice(p * half, (p + 1) * half), slice(cut, d)) for p in range(2)]
+        return jnp.concatenate([chain(kinds, slice(None), slice(0, cut)), jnp.concatenate(last, axis=0)], axis=1)
+
+    total = project((3,))
+    grad = project((0, 1, 2))
     wide = states_ref[...].astype(F32)
     att_ref[...] = (wide + total).astype(BF16)
-    for s in range(shards):
-        for i in range(3):
-            piece = dot_nn(all_s[s, i], wt_s[s, i * n : (i + 1) * n])
-            grad = piece if grad is None else grad + piece
     inv = lax.rsqrt(jnp.mean(wide * wide, axis=-1, keepdims=True) + EPS)
     unit = wide * inv
     gain_out_ref[...] += jnp.sum(grad * unit, axis=0, keepdims=True)
@@ -210,34 +217,45 @@
     qkv_rows = jnp.transpose(qkv_weight, (1, 2, 3, 0)).reshape(3 * n, d)
     wo_rows = output_weight.reshape(n, d)
     size = 4 * n // parts
-    mine = lax.dynamic_slice_in_dim(jnp.concatenate([qkv_rows, wo_rows], axis=0), i_hi * size, size, 0)
-
-    first = [hop_mp(mine, k) for k in range(1, mp)]
-
-    def spread(block):
-        even = {0: block}
-        for r in range(2, parts, 2):
-            even[r] = hop_dp(block, r)
-        blocks = dict(even)
-        for r in range(0, parts, 2):
-            blocks[r ^ 1] = hop_dp(even[r], 1)
-        return [blocks[r] for r in range(parts)]
-
-    near = spread(first[0])
-    rest = spread(jnp.stack(first[1:]))
+    stacked = jnp.concatenate([qkv_rows, wo_rows], axis=0)
+    mine = lax.dynamic_slice_in_dim(stacked, i_hi * size, size, 0)
+    mine_near = lax.dynamic_slice_in_dim(stacked, (i_hi % 4) * n, n, 0)
+
+    near = [hop_mp(mine_near, 1)]
+    first = [hop_mp(mine, k) for k in range(2, mp)]
+    across = hop_dp(near[0], 2)
+    near = [near[0], hop_dp(near[0], 1), across, hop_dp(across, 1)]
+    even = {0: jnp.stack(first)}
+    for r in range(2, parts, 2):
+        even[r] = hop_dp(even[0], r)
+    blocks = dict(even)
+    blocks[1] = hop_dp(even[0], 1)
+    for r in range(2, parts, 2):
+        blocks[r ^ 1] = hop_dp(even[r], 1)
+    rest = [blocks[r] for r in range(parts)]
 
     flat_states = states.reshape(rows, d)
     flat_cot = cotangent.reshape(rows, d)
     gain = norm_gain.reshape(1, d)
     chunk = rows // 4
     grid = rows // chunk
-    scratch = [pltpu.VMEM((chunk, n), BF16) for _ in range(4)]
+    scratch = [pltpu.VMEM((chunk, n), BF16) for _ in range(8)]
+    big_scratch = [pltpu.VMEM((rows // 2, n), BF16) for _ in range(4)]
     flops_in = 2 * rows * d * 4 * n
-    row_spec = pl.BlockSpec((chunk, d), lambda c, *_: (c, 0))
-    all_spec = pl.BlockSpec((4, chunk, n), lambda c, *_: (0, c, 0))
+    big = rows // 2
+
+    def row_of(size):
+        return pl.BlockSpec((size, d), lambda c, *_: (c, 0))
+
+    def all_of(size):
+        return pl.BlockSpec((4, size, n), lambda c, *_: (0, c, 0))
+
     any_spec = pl.BlockSpec(memory_space=pl.ANY)
     all_shape = jax.ShapeDtypeStruct((4, rows, n), BF16)
     row_shape = jax.ShapeDtypeStruct((rows, d), BF16)
+
+    def in_hbm(x):
+        return pltpu.with_memory_space_constraint(x, pltpu.HBM)
 
     def whole(shape):
         return pl.BlockSpec(shape, lambda c, *_: tuple(0 for _ in shape))
@@ -253,10 +271,10 @@
             cost_estimate=pl.CostEstimate(flops=flops, bytes_accessed=rows * d * 8, transcendentals=0))
 
     normed, mcot, all0 = call(
-        functools.partial(own_kernel, seq, heads, width), 3 * flops_in, 24, 1, grid,
-        [row_spec, row_spec, whole((1, d)), whole((3 * n, d)), whole((n, d))],
-        [row_spec, row_spec, all_spec], [row_shape, row_shape, all_shape], scratch,
-    )(hist_len, flat_states, flat_cot, gain, qkv_rows, wo_rows)
+        functools.partial(own_kernel, seq, heads, width), 3 * flops_in, 28, 1, 2,
+        [row_of(big)] * 2 + [whole((1, d)), whole((3 * n, d)), whole((n, d))],
+        [row_of(big)] * 2 + [all_of(big)], [row_shape, row_shape, all_shape], big_scratch,
+    )(hist_len, in_hbm(flat_states), in_hbm(flat_cot), gain, in_hbm(qkv_rows), in_hbm(wo_rows))
 
     piece = (d // parts, 4 * n)
     half = parts // 2
@@ -272,26 +290,27 @@
     arrived = [hop_dp(kept[r].astype(BF16), 2 * r) for r in range(1, half)]
 
     all1, wt1 = call(
-        functools.partial(far_kernel, seq, heads, width, parts), 3 * flops_in, 24, 2, grid,
-        [row_spec, row_spec] + [any_spec] * parts,
-        [all_spec, whole((4 * n, d))], [all_shape, jax.ShapeDtypeStruct((4 * n, d), BF16)],
-        scratch + [pltpu.SemaphoreType.DMA((parts,))],
+        functools.partial(far_kernel, seq, heads, width), 3 * flops_in, 28, 2, 2,
+        [row_of(big)] * 2 + [any_spec] * 4,
+        [all_of(big), whole((4 * n, d))], [all_shape, jax.ShapeDtypeStruct((4 * n, d), BF16)],
+        big_scratch + [pltpu.SemaphoreType.DMA((4,))],
     )(hist_len, meta, normed, mcot, *near)
 
     attended, grad_states, gain_part = call(
-        functools.partial(final_kernel, seq, heads, width, parts, mp), 10 * flops_in, 44, 2, grid,
-        [row_spec, row_spec, row_spec, whole((1, d)), all_spec, all_spec] + [any_spec] * (3 + parts),
-        [row_spec, row_spec, whole((1, d))], [row_shape, row_shape, jax.ShapeDtypeStruct((1, d), F32)],
-        [pltpu.VMEM((mp, 4 * n, d), BF16), pltpu.VMEM((mp, 4, chunk, n), BF16)] + scratch * 2
+        functools.partial(final_kernel, seq, heads, width, parts, mp), 10 * flops_in, 30, 2, grid,
+        [row_of(chunk)] * 3 + [whole((1, d)), all_of(chunk), all_of(chunk)] + [any_spec] * (3 + parts),
+        [row_of(chunk)] * 2 + [whole((1, d))], [row_shape, row_shape, jax.ShapeDtypeStruct((1, d), F32)],
+        [pltpu.VMEM((mp, 4 * n, d), BF16), pltpu.VMEM((mp, 4, chunk, n), BF16)] + scratch
         + [pltpu.SemaphoreType.DMA((3 + (mp - 2) * parts,))],
     )(hist_len, meta, flat_states, normed, mcot, gain, all0, all1, qkv_rows, wo_rows, wt1, *rest)
 
     summed = kept[0]
     for part in arrived:
         summed = summed + part.astype(F32)
-    gain_sum = gain_part
-    for r in range(1, parts):
-        gain_sum = gain_sum + hop_dp(gain_part, r)
+    gain_pair = gain_part + hop_dp(gain_part, 1)
+    gain_sum = gain_pair
+    for r in range(2, parts, 2):
+        gain_sum = gain_sum + hop_dp(gain_pair, r)
     gain_piece = lax.dynamic_slice_in_dim(gain_sum.reshape(d), i_hi * (d // parts), d // parts, 0)
     if low > 1:
         groups = [[hi * low + lo for lo in range(low)] for hi in range(parts)]

time: 115 us -> 104 us (0.904)
  Pallas kernels: 62.3 us -> 46.6 us
  waiting for transfers between devices: 9.65 us -> 23.3 us
  local copies, waits for them, and re-layouts: 15.4 us -> 7.54 us
  starting transfers between devices: 24.8 us -> 19.7 us
  other arithmetic: 1.87 us -> 5.05 us
    pallas_call x1, Pallas kernels: 39.1 us -> 26.7 us  [body(): call(functools.partial(final_kernel, seq, heads, width, parts, mp), 10 *...]
    unnamed x32 -> x30, local copies, waits for them, and re-layouts: 13 us -> 5.13 us
    ppermute x3, waiting for transfers between devices: 2.62 us -> 10.3 us  [hop_mp(): return lax.ppermute(x, 'mp', [(i, i ^ k) for i in range(mp)])]
    ppermute x25 -> x18, waiting for transfers between devices: 7.03 us -> 13 us  [hop_dp(): return lax.ppermute(x, 'dp', [(i, i ^ r * low) for i in range(dp)])]
    ppermute x25 -> x18, starting transfers between devices: 19.1 us -> 13.8 us  [hop_dp(): return lax.ppermute(x, 'dp', [(i, i ^ r * low) for i in range(dp)])]
    pallas_call x2, Pallas kernels: 19.4 us -> 15.3 us  [the longest x1 7.91 us: body(): call(functools.partial(own_kernel, seq, heads, width), 3 * flops_in, 28,...]
    convert_element_type x1, other arithmetic: 0.09 us -> 1.42 us  [body(): arrived = [hop_dp(kept[r].astype(BF16), 2 * r) for r in range(1, half)]]
  transfers between devices with their start and end apart: 28 -> 21, of which waited for: 6 -> 5; matrix products, arithmetic and copies ran while one was open for 2% -> 5% of each run, Pallas kernels for 54% -> 45%
where the time goes in v1:
time: 104 us; the launch traced here: 103 us
  Pallas kernels  46.6 us (45%)
  waiting for transfers between devices  23.3 us (22%)
  starting transfers between devices  19.7 us (19%)
  local copies, waits for them, and re-layouts  7.54 us (7%)
  other arithmetic  5.05 us (5%)
    pallas_call x1, Pallas kernels, body(): call(functools.partial(final_kernel, seq, heads, width, parts, mp), 10 *...  26.7 us
    ppermute x18, starting transfers between devices, hop_dp(): return lax.ppermute(x, 'dp', [(i, i ^ r * low) for i in range(dp)])  13.8 us
    ppermute x18, waiting for transfers between devices, hop_dp(): return lax.ppermute(x, 'dp', [(i, i ^ r * low) for i in range(dp)])  13 us
    ppermute x3, waiting for transfers between devices, hop_mp(): return lax.ppermute(x, 'mp', [(i, i ^ k) for i in range(mp)])  10.3 us
    pallas_call x1, Pallas kernels, body(): call(functools.partial(own_kernel, seq, heads, width), 3 * flops_in, 28,...  7.91 us
    pallas_call x1, Pallas kernels, body(): call(functools.partial(far_kernel, seq, heads, width), 3 * flops_in, 28,...  7.37 us
    ppermute x3, starting transfers between devices, hop_mp(): return lax.ppermute(x, 'mp', [(i, i ^ k) for i in range(mp)])  5.93 us
    unnamed x30, local copies, waits for them, and re-layouts  5.13 us
  transfers between devices with their start and end apart: 21, of which 5 were waited for; matrix products, arithmetic and copies ran while one was open for 5% of the time, Pallas kernels for 45%

profile of v1, /device:TPU:0, one launch (start us, length us, event | category | flops | bytes accessed | tf_op | source)
XLA Modules:
  0.0 103.0 jit_solution(239526407941454795)
XLA Ops:
  0.6 1.9 %fusion = bf16[192,768]{1,0:T(8,128)(2,1)} fusion(s32[]{:T(128)S(6)} %select_n.17, bf16[576,768]{1,0:T(8,128)(2,1)} %bitcast.40, bf16[192,768]{1,0:T(8,128)(2,1)} %bitcast.44), kind=kLoop, calls=%fused_computation.4 | loop fusion | flops 589824 | bytes 1474564 | tf_op jit(solution)/shard_map/concatenate | solution.py:220
  2.5 3.1 %collective-permute-start = (bf16[192,768]{1,0:T(8,128)(2,1)}, bf16[192,768]{1,0:T(8,128)(2,1)}, u32[]{:S(2)}, u32[]{:S(2)}) collective-permute-start(bf16[192,768]{1,0:T(8,128)(2,1)} %fusion), channel_id=1, source_target_pairs={{0,1},{1,0},{2,3},{3,2},{4,5},{5,4},{6,7},{7,6},{8,9},{9,8},{10,11... | collective-permute-start | bytes 884744 | tf_op jit(solution)/shard_map/ppermute | solution.py:215
  7.0 7.9 %shard_map.101 = (bf16[1280,768]{1,0:T(8,128)(2,1)S(1)}, bf16[1280,768]{1,0:T(8,128)(2,1)S(1)}, bf16[4,1280,192]{2,1,0:T(8,128)(2,1)S(1)}) custom-call(s32[16]{0:T(128)S(1)} %copy-done.13, bf16[1280,768]{1,0:T(8,128)(2,1)} %bitcast.48, bf16[1280,768]{1,0:T(8,128)(2,1)} %bitcast.54, f32[1,768]{1,0:T(1,128)S(1)} %reshape.49.gain_ref, ...), custom_call_target="tpu_custom_call" | custom-call | flops 4529848320 | bytes 7864320 | tf_op jit(solution)/shard_map/pallas_call | solution.py:273
  14.9 4.7 %shard_map.104 = (f32[96,768]{1,0:T(8,128)S(1)}, f32[96,768]{1,0:T(8,128)S(1)}, f32[96,768]{1,0:T(8,128)S(1)}, f32[96,768]{1,0:T(8,128)S(1)}, bf16[4,96,768]{2,1,0:T(8,128)(2,1)}) custom-call(s32[2]{0:T(128)S(1)} %pad_add_fusion.meta_ref, bf16[1280,768]{1,0:T(8,128)(2,1)S(1)} %get-tuple-element.18.normed_ref, ...), custom_call_target="tpu_custom_call" | custom-call | flops 1509949440 | bytes 7864320 | tf_op jit(solution)/shard_map/pallas_call | solution.py:281
  22.5 1.6 %collective-permute-start.2 = (bf16[192,768]{1,0:T(8,128)(2,1)}, bf16[192,768]{1,0:T(8,128)(2,1)S(1)}, u32[]{:S(2)}, u32[]{:S(2)}) collective-permute-start(bf16[192,768]{1,0:T(8,128)(2,1)} %collective-permute-done.refs_0_), channel_id=1, source_target_pairs={{0,8},{4,12},{8,0},{12,4},{16,24},{20,28},{24,16},{28,20},{1,9},{5... | collective-permute-start | bytes 884744 | tf_op jit(solution)/shard_map/ppermute | solution.py:212
  24.2 2.6 %collective-permute-start.4 = (bf16[96,768]{1,0:T(8,128)(2,1)S(1)}, bf16[96,768]{1,0:T(8,128)(2,1)S(1)}, u32[]{:S(2)}, u32[]{:S(2)}) collective-permute-start(bf16[96,768]{1,0:T(8,128)(2,1)S(1)} %fusion.8), channel_id=1, source_target_pairs={{0,2},{1,3},{2,0},{3,1},{4,6},{5,7},{6,4},{7,5},{8,10},{9,11},{10,... | collective-permute-start | bytes 442376 | tf_op jit(solution)/shard_map/ppermute | solution.py:215
  27.0 10.3 %collective-permute-done.4 = bf16[96,768]{1,0:T(8,128)(2,1)S(1)} collective-permute-done((bf16[96,768]{1,0:T(8,128)(2,1)S(1)}, bf16[96,768]{1,0:T(8,128)(2,1)S(1)}, u32[]{:S(2)}, u32[]{:S(2)}) %collective-permute-start.4) | collective-permute-done | bytes 147488 | tf_op jit(solution)/shard_map/ppermute | solution.py:215
  37.4 1.6 %collective-permute-start.9 = (bf16[2,96,768]{2,1,0:T(8,128)(2,1)S(1)}, bf16[2,96,768]{2,1,0:T(8,128)(2,1)S(1)}, u32[]{:S(2)}, u32[]{:S(2)}) collective-permute-start(bf16[2,96,768]{2,1,0:T(8,128)(2,1)S(1)} %pad_maximum_fusion.refs_0_), channel_id=1, source_target_pairs={{0,16},{4,20},{8,24},{12,28},{16,0},{20,4},{24,8},{28,12},{1,17},{... | collective-permute-start | bytes 884744 | tf_op jit(solution)/shard_map/ppermute | solution.py:212
  38.9 1.1 %collective-permute-start.11 = (bf16[2,96,768]{2,1,0:T(8,128)(2,1)S(1)}, bf16[2,96,768]{2,1,0:T(8,128)(2,1)S(1)}, u32[]{:S(2)}, u32[]{:S(2)}) collective-permute-start(bf16[2,96,768]{2,1,0:T(8,128)(2,1)S(1)} %pad_maximum_fusion.refs_0_), channel_id=1, source_target_pairs={{0,24},{4,28},{8,16},{12,20},{16,8},{20,12},{24,0},{28,4},{1,25},{... | collective-permute-start | bytes 884744 | tf_op jit(solution)/shard_map/ppermute | solution.py:212
  40.0 0.9 collective-permute-start.7
  41.4 1.4 %fusion.3 = (bf16[96,768]{1,0:T(8,128)(2,1)S(1)}, bf16[96,768]{1,0:T(8,128)(2,1)S(1)}, bf16[96,768]{1,0:T(8,128)(2,1)S(1)}) fusion(f32[96,768]{1,0:T(8,128)} %copy-done.7, bf16[4,96,768]{2,1,0:T(8,128)(2,1)} %collective-permute-done.13, f32[96,768]{1,0:T(8,128)} %copy-done.9, f32[96,768]{1,0:T(8,128)} %copy-done.8), kind=kLoop, calls=%fused_computation.11 | loop fusion | flops 663552 | bytes 1769472 | tf_op jit(solution)/shard_map/convert_element_type | solution.py:290
  42.9 9.8 %collective-permute-done.9.refs_4_ = bf16[2,96,768]{2,1,0:T(8,128)(2,1)S(1)} collective-permute-done((bf16[2,96,768]{2,1,0:T(8,128)(2,1)S(1)}, bf16[2,96,768]{2,1,0:T(8,128)(2,1)S(1)}, u32[]{:S(2)}, u32[]{:S(2)}) %collective-permute-start.9) | collective-permute-done | bytes 294944 | tf_op jit(solution)/shard_map/ppermute | solution.py:212
  54.4 1.4 %collective-permute-start.14 = (bf16[96,768]{1,0:T(8,128)(2,1)S(1)}, bf16[96,768]{1,0:T(8,128)(2,1)S(1)}, u32[]{:S(2)}, u32[]{:S(2)}) collective-permute-start(bf16[96,768]{1,0:T(8,128)(2,1)S(1)} %get-tuple-element.36), channel_id=1, source_target_pairs={{0,8},{4,12},{8,0},{12,4},{16,24},{20,28},{24,16},{28,20},{1,9},{5... | collective-permute-start | bytes 442376 | tf_op jit(solution)/shard_map/ppermute | solution.py:212
  55.8 1.5 %copy-done.4 = bf16[1280,768]{1,0:T(8,128)(2,1)S(1)} copy-done((bf16[1280,768]{1,0:T(8,128)(2,1)S(1)}, bf16[1280,768]{1,0:T(8,128)(2,1)}, u32[]{:S(2)}) %copy-start.4) | copy-done | bytes 1966104
  57.4 7.4 %shard_map.102 = (bf16[4,1280,192]{2,1,0:T(8,128)(2,1)S(1)}, bf16[768,768]{1,0:T(8,128)(2,1)S(1)}) custom-call(s32[16]{0:T(128)S(1)} %copy-done.14, s32[2]{0:T(128)S(1)} %pad_add_fusion.meta_ref, bf16[1280,768]{1,0:T(8,128)(2,1)S(1)} %copy-done.2, bf16[1280,768]{1,0:T(8,128)(2,1)S(1)} %copy-done.4, bf16[192,768]{1,0:T(8,128)(2,1)} %collective-permute-done.refs_0_, ...), custom_call_target="tpu_custom_call" | custom-call | flops 4529848320 | bytes 7864320 | tf_op jit(solution)/shard_map/pallas_call | solution.py:292
  64.8 1.7 %collective-permute-start.15 = (bf16[96,768]{1,0:T(8,128)(2,1)S(1)}, bf16[96,768]{1,0:T(8,128)(2,1)S(1)}, u32[]{:S(2)}, u32[]{:S(2)}) collective-permute-start(bf16[96,768]{1,0:T(8,128)(2,1)S(1)} %get-tuple-element.38), channel_id=1, source_target_pairs={{0,16},{4,20},{8,24},{12,28},{16,0},{20,4},{24,8},{28,12},{1,17},{... | collective-permute-start | bytes 442376 | tf_op jit(solution)/shard_map/ppermute | solution.py:212
  66.9 26.7 %shard_map.103 = (bf16[1280,768]{1,0:T(8,128)(2,1)}, bf16[1280,768]{1,0:T(8,128)(2,1)}, f32[1,768]{1,0:T(1,128)S(1)}) custom-call(s32[16]{0:T(128)S(1)} %copy-done.14, s32[2]{0:T(128)S(1)} %pad_add_fusion.meta_ref, bf16[1280,768]{1,0:T(8,128)(2,1)S(1)} %bitcast.49, bf16[1280,768]{1,0:T(8,128)(2,1)S(1)} %copy-done.2, bf16[1280,768]{1,0:T(8,128)(2,1)S(1)} %copy-done.5, ...), custom_call_target="tpu_custom_call" | custom-call | flops 15099494400 | bytes 7864320 | tf_op jit(solution)/shard_map/pallas_call | solution.py:299
  93.7 1.2 %collective-permute-done.17 = f32[1,768]{1,0:T(1,128)S(1)} collective-permute-done((f32[1,768]{1,0:T(1,128)S(1)}, f32[1,768]{1,0:T(1,128)S(1)}, u32[]{:S(2)}, u32[]{:S(2)}) %collective-permute-start.17) | collective-permute-done | bytes 3104 | tf_op jit(solution)/shard_map/ppermute | solution.py:212
  94.8 1.4 %collective-permute-start.18 = (f32[1,768]{1,0:T(1,128)S(1)}, f32[1,768]{1,0:T(1,128)S(1)}, u32[]{:S(2)}, u32[]{:S(2)}) collective-permute-start(f32[1,768]{1,0:T(1,128)S(1)} %add.55), channel_id=1, source_target_pairs={{0,8},{4,12},{8,0},{12,4},{16,24},{20,28},{24,16},{28,20},{1,9},{5... | collective-permute-start | bytes 9224 | tf_op jit(solution)/shard_map/ppermute | solution.py:212
  96.3 1.7 %collective-permute-start.19 = (f32[1,768]{1,0:T(1,128)S(1)}, f32[1,768]{1,0:T(1,128)S(1)}, u32[]{:S(2)}, u32[]{:S(2)}) collective-permute-start(f32[1,768]{1,0:T(1,128)S(1)} %add.55), channel_id=1, source_target_pairs={{0,16},{4,20},{8,24},{12,28},{16,0},{20,4},{24,8},{28,12},{1,17},{... | collective-permute-start | bytes 9224 | tf_op jit(solution)/shard_map/ppermute | solution.py:212
  98.3 1.0 fusion.7
  99.5 0.9 copy.13
  100.3 0.7 copy.14
  101.1 1.4 %collective-permute-done.20 = f32[1,768]{1,0:T(1,128)S(1)} collective-permute-done((f32[1,768]{1,0:T(1,128)S(1)}, f32[1,768]{1,0:T(1,128)S(1)}, u32[]{:S(2)}, u32[]{:S(2)}) %collective-permute-start.20) | collective-permute-done | bytes 3104 | tf_op jit(solution)/shard_map/ppermute | solution.py:212
  (65 shorter events, 8.5 us)
Async XLA Ops:
  2.5 20.0 %collective-permute-start = (bf16[192,768]{1,0:T(8,128)(2,1)}, bf16[192,768]{1,0:T(8,128)(2,1)}, u32[]{:S(2)}, u32[]{:S(2)}) collective-permute-start(bf16[192,768]{1,0:T(8,128)(2,1)} %fusion), channel_id=1, source_target_pairs={{0,1},{1,0},{2,3},{3,2},{4,5},{5,4},{6,7},{7,6},{8,9},{9,8},{10,11... | collective-permute-start | bytes 884744 | tf_op jit(solution)/shard_map/ppermute | solution.py:215
  22.5 33.3 %copy-start.14 = (s32[16]{0:T(128)S(1)}, s32[16]{0:T(128)}, u32[]{:S(2)}) copy-start(s32[16]{0:T(128)} %len_ref.5) | copy-start | bytes 196
  22.5 18.4 %collective-permute-start.13 = (bf16[4,96,768]{2,1,0:T(8,128)(2,1)}, bf16[4,96,768]{2,1,0:T(8,128)(2,1)}, u32[]{:S(2)}, u32[]{:S(2)}) collective-permute-start(bf16[4,96,768]{2,1,0:T(8,128)(2,1)} %get-tuple-element.26), channel_id=1, source_target_pairs={{0,4},{4,0},{8,12},{12,8},{16,20},{20,16},{24,28},{28,24},{1,5},{5... | collective-permute-start | bytes 1769480 | tf_op jit(solution)/shard_map/ppermute | solution.py:212
  22.5 33.3 %copy-start.2 = (bf16[1280,768]{1,0:T(8,128)(2,1)S(1)}, bf16[1280,768]{1,0:T(8,128)(2,1)}, u32[]{:S(2)}) copy-start(bf16[1280,768]{1,0:T(8,128)(2,1)} %copy-done.1) | copy-start | bytes 5898244
  22.5 18.4 %collective-permute-start.2 = (bf16[192,768]{1,0:T(8,128)(2,1)}, bf16[192,768]{1,0:T(8,128)(2,1)S(1)}, u32[]{:S(2)}, u32[]{:S(2)}) collective-permute-start(bf16[192,768]{1,0:T(8,128)(2,1)} %collective-permute-done.refs_0_), channel_id=1, source_target_pairs={{0,8},{4,12},{8,0},{12,4},{16,24},{20,28},{24,16},{28,20},{1,9},{5... | collective-permute-start | bytes 884744 | tf_op jit(solution)/shard_map/ppermute | solution.py:212
  24.2 13.2 %collective-permute-start.4 = (bf16[96,768]{1,0:T(8,128)(2,1)S(1)}, bf16[96,768]{1,0:T(8,128)(2,1)S(1)}, u32[]{:S(2)}, u32[]{:S(2)}) collective-permute-start(bf16[96,768]{1,0:T(8,128)(2,1)S(1)} %fusion.8), channel_id=1, source_target_pairs={{0,2},{1,3},{2,0},{3,1},{4,6},{5,7},{6,4},{7,5},{8,10},{9,11},{10,... | collective-permute-start | bytes 442376 | tf_op jit(solution)/shard_map/ppermute | solution.py:215
  26.8 10.5 %collective-permute-start.5 = (bf16[96,768]{1,0:T(8,128)(2,1)S(1)}, bf16[96,768]{1,0:T(8,128)(2,1)S(1)}, u32[]{:S(2)}, u32[]{:S(2)}) collective-permute-start(bf16[96,768]{1,0:T(8,128)(2,1)S(1)} %fusion.8), channel_id=1, source_target_pairs={{0,3},{1,2},{2,1},{3,0},{4,7},{5,6},{6,5},{7,4},{8,11},{9,10},{10,... | collective-permute-start | bytes 442376 | tf_op jit(solution)/shard_map/ppermute | solution.py:215
  37.4 15.3 %collective-permute-start.9 = (bf16[2,96,768]{2,1,0:T(8,128)(2,1)S(1)}, bf16[2,96,768]{2,1,0:T(8,128)(2,1)S(1)}, u32[]{:S(2)}, u32[]{:S(2)}) collective-permute-start(bf16[2,96,768]{2,1,0:T(8,128)(2,1)S(1)} %pad_maximum_fusion.refs_0_), channel_id=1, source_target_pairs={{0,16},{4,20},{8,24},{12,28},{16,0},{20,4},{24,8},{28,12},{1,17},{... | collective-permute-start | bytes 884744 | tf_op jit(solution)/shard_map/ppermute | solution.py:212
  38.9 13.7 %collective-permute-start.11 = (bf16[2,96,768]{2,1,0:T(8,128)(2,1)S(1)}, bf16[2,96,768]{2,1,0:T(8,128)(2,1)S(1)}, u32[]{:S(2)}, u32[]{:S(2)}) collective-permute-start(bf16[2,96,768]{2,1,0:T(8,128)(2,1)S(1)} %pad_maximum_fusion.refs_0_), channel_id=1, source_target_pairs={{0,24},{4,28},{8,16},{12,20},{16,8},{20,12},{24,0},{28,4},{1,25},{... | collective-permute-start | bytes 884744 | tf_op jit(solution)/shard_map/ppermute | solution.py:212
  40.0 13.8 %collective-permute-start.7 = (bf16[2,96,768]{2,1,0:T(8,128)(2,1)S(1)}, bf16[2,96,768]{2,1,0:T(8,128)(2,1)S(1)}, u32[]{:S(2)}, u32[]{:S(2)}) collective-permute-start(bf16[2,96,768]{2,1,0:T(8,128)(2,1)S(1)} %pad_maximum_fusion.refs_0_), channel_id=1, source_target_pairs={{0,8},{4,12},{8,0},{12,4},{16,24},{20,28},{24,16},{28,20},{1,9},{5... | collective-permute-start | bytes 884744 | tf_op jit(solution)/shard_map/ppermute | solution.py:212
  40.9 12.9 %collective-permute-start.1 = (bf16[192,768]{1,0:T(8,128)(2,1)}, bf16[192,768]{1,0:T(8,128)(2,1)S(1)}, u32[]{:S(2)}, u32[]{:S(2)}) collective-permute-start(bf16[192,768]{1,0:T(8,128)(2,1)} %collective-permute-done.refs_0_), channel_id=1, source_target_pairs={{0,4},{4,0},{8,12},{12,8},{16,20},{20,16},{24,28},{28,24},{1,5},{5... | collective-permute-start | bytes 884744 | tf_op jit(solution)/shard_map/ppermute | solution.py:212
  40.9 13.4 %collective-permute-start.3 = (bf16[192,768]{1,0:T(8,128)(2,1)S(1)}, bf16[192,768]{1,0:T(8,128)(2,1)S(1)}, u32[]{:S(2)}, u32[]{:S(2)}) collective-permute-start(bf16[192,768]{1,0:T(8,128)(2,1)S(1)} %collective-permute-done.2.refs_2_), channel_id=1, source_target_pairs={{0,4},{4,0},{8,12},{12,8},{16,20},{20,16},{24,28},{28,24},{1,5},{5... | collective-permute-start | bytes 884744 | tf_op jit(solution)/shard_map/ppermute | solution.py:212
  52.6 12.1 %collective-permute-start.6 = (bf16[2,96,768]{2,1,0:T(8,128)(2,1)S(1)}, bf16[2,96,768]{2,1,0:T(8,128)(2,1)S(1)}, u32[]{:S(2)}, u32[]{:S(2)}) collective-permute-start(bf16[2,96,768]{2,1,0:T(8,128)(2,1)S(1)} %pad_maximum_fusion.refs_0_), channel_id=1, source_target_pairs={{0,4},{4,0},{8,12},{12,8},{16,20},{20,16},{24,28},{28,24},{1,5},{5... | collective-permute-start | bytes 884744 | tf_op jit(solution)/shard_map/ppermute | solution.py:212
  52.6 13.9 %collective-permute-start.10 = (bf16[2,96,768]{2,1,0:T(8,128)(2,1)S(1)}, bf16[2,96,768]{2,1,0:T(8,128)(2,1)S(1)}, u32[]{:S(2)}, u32[]{:S(2)}) collective-permute-start(bf16[2,96,768]{2,1,0:T(8,128)(2,1)S(1)} %collective-permute-done.9.refs_4_), channel_id=1, source_target_pairs={{0,4},{4,0},{8,12},{12,8},{16,20},{20,16},{24,28},{28,24},{1,5},{5... | collective-permute-start | bytes 884744 | tf_op jit(solution)/shard_map/ppermute | solution.py:212
  53.9 13.0 %collective-permute-start.12 = (bf16[2,96,768]{2,1,0:T(8,128)(2,1)S(1)}, bf16[2,96,768]{2,1,0:T(8,128)(2,1)S(1)}, u32[]{:S(2)}, u32[]{:S(2)}) collective-permute-start(bf16[2,96,768]{2,1,0:T(8,128)(2,1)S(1)} %collective-permute-done.11.refs_6_), channel_id=1, source_target_pairs={{0,4},{4,0},{8,12},{12,8},{16,20},{20,16},{24,28},{28,24},{1,5},{5... | collective-permute-start | bytes 884744 | tf_op jit(solution)/shard_map/ppermute | solution.py:212
  53.9 13.0 %collective-permute-start.8 = (bf16[2,96,768]{2,1,0:T(8,128)(2,1)S(1)}, bf16[2,96,768]{2,1,0:T(8,128)(2,1)S(1)}, u32[]{:S(2)}, u32[]{:S(2)}) collective-permute-start(bf16[2,96,768]{2,1,0:T(8,128)(2,1)S(1)} %collective-permute-done.7.refs_2_), channel_id=1, source_target_pairs={{0,4},{4,0},{8,12},{12,8},{16,20},{20,16},{24,28},{28,24},{1,5},{5... | collective-permute-start | bytes 884744 | tf_op jit(solution)/shard_map/ppermute | solution.py:212
  54.4 43.6 %collective-permute-start.14 = (bf16[96,768]{1,0:T(8,128)(2,1)S(1)}, bf16[96,768]{1,0:T(8,128)(2,1)S(1)}, u32[]{:S(2)}, u32[]{:S(2)}) collective-permute-start(bf16[96,768]{1,0:T(8,128)(2,1)S(1)} %get-tuple-element.36), channel_id=1, source_target_pairs={{0,8},{4,12},{8,0},{12,4},{16,24},{20,28},{24,16},{28,20},{1,9},{5... | collective-permute-start | bytes 442376 | tf_op jit(solution)/shard_map/ppermute | solution.py:212
  64.8 33.6 %collective-permute-start.15 = (bf16[96,768]{1,0:T(8,128)(2,1)S(1)}, bf16[96,768]{1,0:T(8,128)(2,1)S(1)}, u32[]{:S(2)}, u32[]{:S(2)}) collective-permute-start(bf16[96,768]{1,0:T(8,128)(2,1)S(1)} %get-tuple-element.38), channel_id=1, source_target_pairs={{0,16},{4,20},{8,24},{12,28},{16,0},{20,4},{24,8},{28,12},{1,17},{... | collective-permute-start | bytes 442376 | tf_op jit(solution)/shard_map/ppermute | solution.py:212
  66.5 31.8 %collective-permute-start.16 = (bf16[96,768]{1,0:T(8,128)(2,1)S(1)}, bf16[96,768]{1,0:T(8,128)(2,1)S(1)}, u32[]{:S(2)}, u32[]{:S(2)}) collective-permute-start(bf16[96,768]{1,0:T(8,128)(2,1)S(1)} %get-tuple-element.37), channel_id=1, source_target_pairs={{0,24},{4,28},{8,16},{12,20},{16,8},{20,12},{24,0},{28,4},{1,25},{... | collective-permute-start | bytes 442376 | tf_op jit(solution)/shard_map/ppermute | solution.py:212
  66.9 31.4 %copy-start.11 = (f32[96,768]{1,0:T(8,128)S(1)}, f32[96,768]{1,0:T(8,128)}, u32[]{:S(2)}) copy-start(f32[96,768]{1,0:T(8,128)} %copy-done.10) | copy-start | bytes 884740
  93.6 1.2 %collective-permute-start.17 = (f32[1,768]{1,0:T(1,128)S(1)}, f32[1,768]{1,0:T(1,128)S(1)}, u32[]{:S(2)}, u32[]{:S(2)}) collective-permute-start(f32[1,768]{1,0:T(1,128)S(1)} %get-tuple-element.30), channel_id=1, source_target_pairs={{0,4},{4,0},{8,12},{12,8},{16,20},{20,16},{24,28},{28,24},{1,5},{5... | collective-permute-start | bytes 9224 | tf_op jit(solution)/shard_map/ppermute | solution.py:212
  94.8 6.2 %collective-permute-start.18 = (f32[1,768]{1,0:T(1,128)S(1)}, f32[1,768]{1,0:T(1,128)S(1)}, u32[]{:S(2)}, u32[]{:S(2)}) collective-permute-start(f32[1,768]{1,0:T(1,128)S(1)} %add.55), channel_id=1, source_target_pairs={{0,8},{4,12},{8,0},{12,4},{16,24},{20,28},{24,16},{28,20},{1,9},{5... | collective-permute-start | bytes 9224 | tf_op jit(solution)/shard_map/ppermute | solution.py:212
  96.3 4.8 %collective-permute-start.19 = (f32[1,768]{1,0:T(1,128)S(1)}, f32[1,768]{1,0:T(1,128)S(1)}, u32[]{:S(2)}, u32[]{:S(2)}) collective-permute-start(f32[1,768]{1,0:T(1,128)S(1)} %add.55), channel_id=1, source_target_pairs={{0,16},{4,20},{8,24},{12,28},{16,0},{20,4},{24,8},{28,12},{1,17},{... | collective-permute-start | bytes 9224 | tf_op jit(solution)/shard_map/ppermute | solution.py:212
  97.9 4.5 %collective-permute-start.20 = (f32[1,768]{1,0:T(1,128)S(1)}, f32[1,768]{1,0:T(1,128)S(1)}, u32[]{:S(2)}, u32[]{:S(2)}) collective-permute-start(f32[1,768]{1,0:T(1,128)S(1)} %add.55), channel_id=1, source_target_pairs={{0,24},{4,28},{8,16},{12,20},{16,8},{20,12},{24,0},{28,4},{1,25},{... | collective-permute-start | bytes 9224 | tf_op jit(solution)/shard_map/ppermute | solution.py:212
  (12 other events, 52.2 us)

commit v2 on v1

--- a/solution.py
+++ b/solution.py
@@ -24,6 +24,20 @@
 
 def dot_tn(a, b):
     return lax.dot_general(a, b, (((0,), (0,)), ((), ())), preferred_element_type=F32)
+
+
+def project(pairs):
+    def chain(rows, columns):
+        out = None
+        for left, right in pairs:
+            part = dot_nn(left[rows], right[:, columns])
+            out = part if out is None else out + part
+        return out
+
+    count, d = pairs[0][0].shape[0], pairs[0][1].shape[1]
+    cut, half = d - 256, count // 2
+    last = [chain(slice(p * half, (p + 1) * half), slice(cut, d)) for p in range(2)]
+    return jnp.concatenate([chain(slice(None), slice(0, cut)), jnp.concatenate(last, axis=0)], axis=1)
 
 
 def attention(refs, out_ref, valid, heads, width):
@@ -78,7 +92,7 @@
 
 
 def own_kernel(seq, heads, width, len_ref, states_ref, cot_ref, gain_ref, qkv_ref, wo_ref,
-               normed_ref, mcot_ref, out_ref, *scratch):
+               normed_ref, mcot_ref, out_ref, gain_out_ref, *scratch):
     wide = states_ref[...].astype(F32)
     inv = lax.rsqrt(jnp.mean(wide * wide, axis=-1, keepdims=True) + EPS)
     normed = (wide * inv * gain_ref[...]).astype(BF16)
@@ -91,18 +105,25 @@
     shard_body(len_ref, normed, mcot, qkv_ref[:n], qkv_ref[n : 2 * n], qkv_ref[2 * n : 3 * n], wo_ref[...],
                out_ref.at[:], scratch, seq, heads, width)
 
+    @pl.when(pl.program_id(0) == 0)
+    def _():
+        gain_out_ref[...] = jnp.zeros_like(gain_out_ref)
+
+    grad = project([(out_ref.at[i], qkv_ref.at[i * n : (i + 1) * n]) for i in range(3)])
+    gain_out_ref[...] += jnp.sum(grad * (states_ref[...].astype(F32) * inv), axis=0, keepdims=True)
+
 
 def far_kernel(seq, heads, width, len_ref, meta_ref, normed_ref, mcot_ref, *refs):
-    blocks = refs[:4]
-    out_ref, wt_ref, q_s, k_s, v_s, g_s, sems = refs[4:]
+    blocks = refs[:2]
+    out_ref, wt_ref, q_s, k_s, v_s, g_s, sems = refs[2:]
     n = heads * width
 
     @pl.when(pl.program_id(0) == 0)
     def _():
         copies = []
-        for r in range(4):
-            place = pl.multiple_of(((meta_ref[1] % 4) ^ r) * n, 8)
-            copies.append(pltpu.make_async_copy(blocks[r], wt_ref.at[pl.ds(place, n)], sems.at[r]))
+        for r in range(2):
+            place = pl.multiple_of(((meta_ref[1] % 2) ^ r) * 2 * n, 8)
+            copies.append(pltpu.make_async_copy(blocks[r], wt_ref.at[pl.ds(place, 2 * n)], sems.at[r]))
         for copy in copies:
             copy.start()
         for copy in copies:
@@ -139,8 +160,8 @@
 def final_kernel(seq, heads, width, parts, shards, len_ref, meta_ref, states_ref, normed_ref, mcot_ref, gain_ref,
                  all0_ref, all1_ref, qkv_ref, wo_ref, wt1_ref, *refs):
     blocks = refs[:parts]
-    att_ref, grad_ref, gain_out_ref, wt_s, all_s = refs[parts : parts + 5]
-    scratch, sems = refs[parts + 5 : -1], refs[-1]
+    att_ref, grad_ref, wt_s, all_s = refs[parts : parts + 4]
+    scratch, sems = refs[parts + 4 : -1], refs[-1]
     n = heads * width
     size = 4 * n // parts
     own = meta_ref[0]
@@ -161,37 +182,28 @@
             copy.start()
         for copy in copies:
             copy.wait()
-        gain_out_ref[...] = jnp.zeros_like(gain_out_ref)
 
     all_s[own] = all0_ref[...]
     all_s[own ^ 1] = all1_ref[...]
     normed, mcot = normed_ref[...], mcot_ref[...]
+    count = normed.shape[0] // seq
+    valid = [LEVELS * len_ref[pl.program_id(0) * count + b] for b in range(count)]
     for k in range(2, shards):
-        w = [wt_s[own ^ k, i * n : (i + 1) * n] for i in range(4)]
-        shard_body(len_ref, normed, mcot, w[0], w[1], w[2], w[3],
-                   all_s.at[own ^ k], scratch[4 * (k % 2) : 4 * (k % 2) + 4], seq, heads, width)
-
-    def chain(kinds, rows, columns):
-        out = None
-        for s in range(shards):
-            for i in kinds:
-                piece = dot_nn(all_s[s, i, rows], wt_s[s, i * n : (i + 1) * n, columns])
-                out = piece if out is None else out + piece
-        return out
-
-    def project(kinds):
-        count, d = states_ref.shape
-        cut, half = d - 256, count // 2
-        last = [chain(kinds, slice(p * half, (p + 1) * half), slice(cut, d)) for p in range(2)]
-        return jnp.concatenate([chain(kinds, slice(None), slice(0, cut)), jnp.concatenate(last, axis=0)], axis=1)
-
-    total = project((3,))
-    grad = project((0, 1, 2))
+        for i in range(4):
+            left = mcot if i == 3 else normed
+            scratch[4 * (k % 2) + i][...] = dot_nt(left, wt_s[own ^ k, i * n : (i + 1) * n]).astype(BF16)
+    for k in range(2, shards):
+        attention(scratch[4 * (k % 2) : 4 * (k % 2) + 4], all_s.at[own ^ k], valid, heads, width)
+
+    def piece(kind, shard):
+        return all_s.at[shard, kind], wt_s.at[shard, kind * n : (kind + 1) * n]
+
+    total = project([piece(3, s) for s in range(shards)])
+    grad = project([piece(i, s) for s in range(shards) for i in range(3)])
     wide = states_ref[...].astype(F32)
     att_ref[...] = (wide + total).astype(BF16)
     inv = lax.rsqrt(jnp.mean(wide * wide, axis=-1, keepdims=True) + EPS)
     unit = wide * inv
-    gain_out_ref[...] += jnp.sum(grad * unit, axis=0, keepdims=True)
     unit_grad = grad * gain_ref[...]
     corr = jnp.mean(unit_grad * unit, axis=-1, keepdims=True)
     grad_ref[...] = (mcot.astype(F32) + inv * (unit_grad - unit * corr)).astype(BF16)
@@ -219,12 +231,11 @@
     size = 4 * n // parts
     stacked = jnp.concatenate([qkv_rows, wo_rows], axis=0)
     mine = lax.dynamic_slice_in_dim(stacked, i_hi * size, size, 0)
-    mine_near = lax.dynamic_slice_in_dim(stacked, (i_hi % 4) * n, n, 0)
+    mine_near = lax.dynamic_slice_in_dim(stacked, (i_hi % 2) * 2 * n, 2 * n, 0)
 
     near = [hop_mp(mine_near, 1)]
     first = [hop_mp(mine, k) for k in range(2, mp)]
-    across = hop_dp(near[0], 2)
-    near = [near[0], hop_dp(near[0], 1), across, hop_dp(across, 1)]
+    near.append(hop_dp(near[0], 1))
     even = {0: jnp.stack(first)}
     for r in range(2, parts, 2):
         even[r] = hop_dp(even[0], r)
@@ -270,10 +281,11 @@
                 dimension_semantics=("arbitrary",), vmem_limit_bytes=vmem * 1024 * 1024),
             cost_estimate=pl.CostEstimate(flops=flops, bytes_accessed=rows * d * 8, transcendentals=0))
 
-    normed, mcot, all0 = call(
+    normed, mcot, all0, gain_part = call(
         functools.partial(own_kernel, seq, heads, width), 3 * flops_in, 28, 1, 2,
         [row_of(big)] * 2 + [whole((1, d)), whole((3 * n, d)), whole((n, d))],
-        [row_of(big)] * 2 + [all_of(big)], [row_shape, row_shape, all_shape], big_scratch,
+        [row_of(big)] * 2 + [all_of(big), whole((1, d))],
+        [row_shape, row_shape, all_shape, jax.ShapeDtypeStruct((1, d), F32)], big_scratch,
     )(hist_len, in_hbm(flat_states), in_hbm(flat_cot), gain, in_hbm(qkv_rows), in_hbm(wo_rows))
 
     piece = (d // parts, 4 * n)
@@ -285,32 +297,41 @@
         [jax.ShapeDtypeStruct(piece, F32)] * half + [jax.ShapeDtypeStruct((half,) + piece, BF16)],
         [pltpu.VMEM((4, parts, d // parts, n), F32)],
     )(meta, normed, mcot, all0)
-    pair = hop_dp(sent, 1)
-    kept = [kept[r] + pair[r].astype(F32) for r in range(half)]
-    arrived = [hop_dp(kept[r].astype(BF16), 2 * r) for r in range(1, half)]
-
+    others = [hop_mp(gain_part, k) for k in range(1, mp)]
     all1, wt1 = call(
         functools.partial(far_kernel, seq, heads, width), 3 * flops_in, 28, 2, 2,
-        [row_of(big)] * 2 + [any_spec] * 4,
+        [row_of(big)] * 2 + [any_spec] * 2,
         [all_of(big), whole((4 * n, d))], [all_shape, jax.ShapeDtypeStruct((4 * n, d), BF16)],
-        big_scratch + [pltpu.SemaphoreType.DMA((4,))],
+        big_scratch + [pltpu.SemaphoreType.DMA((2,))],
     )(hist_len, meta, normed, mcot, *near)
 
-    attended, grad_states, gain_part = call(
+    all1, others = lax.optimization_barrier((all1, others))
+    level = [gain_part] + others
+    while len(level) > 1:
+        level = [level[i] + level[i + 1] for i in range(0, len(level), 2)]
+    gain_part = level[0]
+    pair = hop_dp(sent, 1)
+    gain_part = gain_part + hop_dp(gain_part, 1)
+    kept = [kept[r] + pair[r].astype(F32) for r in range(half)]
+    rounded = lax.reduce_precision(gain_part, 8, 7)
+    tail = jnp.concatenate([rounded, gain_part - rounded, jnp.zeros((14, d), F32)], axis=0).astype(BF16)
+    arrived = [
+        hop_dp(jnp.concatenate([kept[r].astype(BF16), tail], axis=0), 2 * r) for r in range(1, half)
+    ]
+
+    attended, grad_states = call(
         functools.partial(final_kernel, seq, heads, width, parts, mp), 10 * flops_in, 30, 2, grid,
         [row_of(chunk)] * 3 + [whole((1, d)), all_of(chunk), all_of(chunk)] + [any_spec] * (3 + parts),
-        [row_of(chunk)] * 2 + [whole((1, d))], [row_shape, row_shape, jax.ShapeDtypeStruct((1, d), F32)],
+        [row_of(chunk)] * 2, [row_shape, row_shape],
         [pltpu.VMEM((mp, 4 * n, d), BF16), pltpu.VMEM((mp, 4, chunk, n), BF16)] + scratch
         + [pltpu.SemaphoreType.DMA((3 + (mp - 2) * parts,))],
     )(hist_len, meta, flat_states, normed, mcot, gain, all0, all1, qkv_rows, wo_rows, wt1, *rest)
 
-    summed = kept[0]
+    attended, arrived = lax.optimization_barrier((attended, arrived))
+    summed, gain_sum = kept[0], gain_part
     for part in arrived:
-        summed = summed + part.astype(F32)
-    gain_pair = gain_part + hop_dp(gain_part, 1)
-    gain_sum = gain_pair
-    for r in range(2, parts, 2):
-        gain_sum = gain_sum + hop_dp(gain_pair, r)
+        summed = summed + part[: d // parts].astype(F32)
+        gain_sum = gain_sum + (part[d // parts].astype(F32) + part[d // parts + 1].astype(F32))
     gain_piece = lax.dynamic_slice_in_dim(gain_sum.reshape(d), i_hi * (d // parts), d // parts, 0)
     if low > 1:
         groups = [[hi * low + lo for lo in range(low)] for hi in range(parts)]

time: 104 us -> 106 us (1.019)
  local copies, waits for them, and re-layouts: 7.54 us -> 8.81 us
  Pallas kernels: 46.6 us -> 47.8 us
    ppermute x3 -> x6, waiting for transfers between devices: 10.3 us -> 17.2 us  [hop_mp(): return lax.ppermute(x, 'mp', [(i, i ^ k) for i in range(mp)])]
    ppermute x18 -> x13, waiting for transfers between devices: 13 us -> 7.01 us  [hop_dp(): return lax.ppermute(x, 'dp', [(i, i ^ r * low) for i in range(dp)])]
    ppermute x3 -> x6, starting transfers between devices: 5.93 us -> 11.3 us  [hop_mp(): return lax.ppermute(x, 'mp', [(i, i ^ k) for i in range(mp)])]
    ppermute x18 -> x13, starting transfers between devices: 13.8 us -> 8.69 us  [hop_dp(): return lax.ppermute(x, 'dp', [(i, i ^ r * low) for i in range(dp)])]
    pallas_call x1, Pallas kernels: 7.91 us -> 10.1 us  [body(): call(functools.partial(own_kernel, seq, heads, width), 3 * flops_in, 28,...]
    convert_element_type x1, other arithmetic: 1.42 us -> 0.11 us  [body(): kept[r].astype(BF16)]
    unnamed x30 -> x22, local copies, waits for them, and re-layouts: 5.13 us -> 6.31 us
  transfers between devices with their start and end apart: 21 -> 19, of which waited for: 5 -> 4; matrix products, arithmetic and copies ran while one was open for 5% -> 3% of each run, Pallas kernels for 45% -> 45%
where the time goes in v2:
time: 106 us
  Pallas kernels  47.8 us (45%)
  waiting for transfers between devices  24.2 us (23%)
  starting transfers between devices  20 us (19%)
  local copies, waits for them, and re-layouts  8.81 us (8%)
  other arithmetic  4.18 us (4%)
    pallas_call x1, Pallas kernels, body(): call(functools.partial(final_kernel, seq, heads, width, parts, mp), 10 *...  26.5 us
    ppermute x6, waiting for transfers between devices, hop_mp(): return lax.ppermute(x, 'mp', [(i, i ^ k) for i in range(mp)])  17.2 us
    ppermute x6, starting transfers between devices, hop_mp(): return lax.ppermute(x, 'mp', [(i, i ^ k) for i in range(mp)])  11.3 us
    pallas_call x1, Pallas kernels, body(): call(functools.partial(own_kernel, seq, heads, width), 3 * flops_in, 28,...  10.1 us
    ppermute x13, starting transfers between devices, hop_dp(): return lax.ppermute(x, 'dp', [(i, i ^ r * low) for i in range(dp)])  8.69 us
    pallas_call x1, Pallas kernels, body(): call(functools.partial(far_kernel, seq, heads, width), 3 * flops_in, 28,...  7.37 us
    ppermute x13, waiting for transfers between devices, hop_dp(): return lax.ppermute(x, 'dp', [(i, i ^ r * low) for i in range(dp)])  7.01 us
    unnamed x22, local copies, waits for them, and re-layouts  6.31 us
  transfers between devices with their start and end apart: 19, of which 4 were waited for; matrix products, arithmetic and copies ran while one was open for 3% of the time, Pallas kernels for 45%

profile of v2, /device:TPU:0, one launch (start us, length us, event | category | flops | bytes accessed | tf_op | source)
XLA Modules:
  0.0 106.0 jit_solution(11162375847747103748)
XLA Ops:
  0.6 1.4 %fusion = bf16[384,768]{1,0:T(8,128)(2,1)S(1)} fusion(s32[]{:T(128)S(6)} %select_n.17, bf16[576,768]{1,0:T(8,128)(2,1)} %bitcast.40, bf16[192,768]{1,0:T(8,128)(2,1)} %bitcast.44), kind=kLoop, calls=%fused_computation.4 | loop fusion | flops 1179648 | bytes 1769476 | tf_op jit(solution)/shard_map/concatenate | solution.py:232
  2.0 3.1 %collective-permute-start = (bf16[384,768]{1,0:T(8,128)(2,1)S(1)}, bf16[384,768]{1,0:T(8,128)(2,1)}, u32[]{:S(2)}, u32[]{:S(2)}) collective-permute-start(bf16[384,768]{1,0:T(8,128)(2,1)S(1)} %fusion), channel_id=1, source_target_pairs={{0,1},{1,0},{2,3},{3,2},{4,5},{5,4},{6,7},{7,6},{8,9},{9,8},{10,11... | collective-permute-start | bytes 1769480 | tf_op jit(solution)/shard_map/ppermute | solution.py:227
  5.8 12.7 %collective-permute-done.refs_0_ = bf16[384,768]{1,0:T(8,128)(2,1)} collective-permute-done((bf16[384,768]{1,0:T(8,128)(2,1)S(1)}, bf16[384,768]{1,0:T(8,128)(2,1)}, u32[]{:S(2)}, u32[]{:S(2)}) %collective-permute-start) | collective-permute-done | bytes 589856 | tf_op jit(solution)/shard_map/ppermute | solution.py:227
  19.2 10.1 %shard_map.101 = (bf16[1280,768]{1,0:T(8,128)(2,1)S(1)}, bf16[1280,768]{1,0:T(8,128)(2,1)S(1)}, bf16[4,1280,192]{2,1,0:T(8,128)(2,1)S(1)}, f32[1,768]{1,0:T(1,128)S(1)}) custom-call(s32[16]{0:T(128)S(1)} %copy-done.9, bf16[1280,768]{1,0:T(8,128)(2,1)} %bitcast.48, bf16[1280,768]{1,0:T(8,128)(2,1)} %bitcast.52, f32[1,768]{1,0:T(1,128)S(1)} %reshape.49.gain_ref, ...), custom_call_target="tpu_custom_call" | custom-call | flops 4529848320 | bytes 7864320 | tf_op jit(solution)/shard_map/pallas_call | solution.py:284
  29.3 1.3 %copy-done.1 = bf16[1280,768]{1,0:T(8,128)(2,1)} copy-done((bf16[1280,768]{1,0:T(8,128)(2,1)}, bf16[1280,768]{1,0:T(8,128)(2,1)S(1)}, u32[]{:S(2)}) %copy-start.1) | copy-done | bytes 1966104
  30.6 1.3 %copy-done.4 = bf16[1280,768]{1,0:T(8,128)(2,1)} copy-done((bf16[1280,768]{1,0:T(8,128)(2,1)}, bf16[1280,768]{1,0:T(8,128)(2,1)S(1)}, u32[]{:S(2)}) %copy-start.4) | copy-done | bytes 1966104
  31.9 1.7 %collective-permute-start.2 = (f32[1,768]{1,0:T(1,128)S(1)}, f32[1,768]{1,0:T(1,128)S(1)}, u32[]{:S(2)}, u32[]{:S(2)}) collective-permute-start(f32[1,768]{1,0:T(1,128)S(1)} %get-tuple-element.30), channel_id=1, source_target_pairs={{0,1},{1,0},{2,3},{3,2},{4,5},{5,4},{6,7},{7,6},{8,9},{9,8},{10,11... | collective-permute-start | bytes 9224 | tf_op jit(solution)/shard_map/ppermute | solution.py:227
  33.6 2.6 %collective-permute-start.3 = (f32[1,768]{1,0:T(1,128)S(1)}, f32[1,768]{1,0:T(1,128)S(1)}, u32[]{:S(2)}, u32[]{:S(2)}) collective-permute-start(f32[1,768]{1,0:T(1,128)S(1)} %get-tuple-element.30), channel_id=1, source_target_pairs={{0,2},{1,3},{2,0},{3,1},{4,6},{5,7},{6,4},{7,5},{8,10},{9,11},{10,... | collective-permute-start | bytes 9224 | tf_op jit(solution)/shard_map/ppermute | solution.py:227
  37.0 1.9 %collective-permute-start.5 = (bf16[96,768]{1,0:T(8,128)(2,1)}, bf16[96,768]{1,0:T(8,128)(2,1)}, u32[]{:S(2)}, u32[]{:S(2)}) collective-permute-start(bf16[96,768]{1,0:T(8,128)(2,1)} %fusion.11), channel_id=1, source_target_pairs={{0,2},{1,3},{2,0},{3,1},{4,6},{5,7},{6,4},{7,5},{8,10},{9,11},{10,... | collective-permute-start | bytes 442376 | tf_op jit(solution)/shard_map/ppermute | solution.py:227
  39.0 1.5 %copy-done.2 = bf16[1280,768]{1,0:T(8,128)(2,1)S(1)} copy-done((bf16[1280,768]{1,0:T(8,128)(2,1)S(1)}, bf16[1280,768]{1,0:T(8,128)(2,1)}, u32[]{:S(2)}) %copy-start.2) | copy-done | bytes 1966104
  40.6 1.5 %copy-done.5 = bf16[1280,768]{1,0:T(8,128)(2,1)S(1)} copy-done((bf16[1280,768]{1,0:T(8,128)(2,1)S(1)}, bf16[1280,768]{1,0:T(8,128)(2,1)}, u32[]{:S(2)}) %copy-start.5) | copy-done | bytes 1966104
  42.1 3.8 %shard_map.104 = (f32[96,768]{1,0:T(8,128)S(1)}, f32[96,768]{1,0:T(8,128)S(1)}, f32[96,768]{1,0:T(8,128)S(1)}, f32[96,768]{1,0:T(8,128)S(1)}, bf16[4,96,768]{2,1,0:T(8,128)(2,1)S(1)}) custom-call(s32[2]{0:T(128)S(1)} %pad_add_fusion.meta_ref, bf16[1280,768]{1,0:T(8,128)(2,1)S(1)} %copy-done.2, bf16[1280,768]{1,0:T(8,128)(2,1)S(1)} %copy-done.5, ...), custom_call_target="tpu_custom_call" | custom-call | flops 1509949440 | bytes 7864320 | tf_op jit(solution)/shard_map/pallas_call | solution.py:293
  46.0 2.0 %collective-permute-start.4 = (f32[1,768]{1,0:T(1,128)S(1)}, f32[1,768]{1,0:T(1,128)S(1)}, u32[]{:S(2)}, u32[]{:S(2)}) collective-permute-start(f32[1,768]{1,0:T(1,128)S(1)} %get-tuple-element.30), channel_id=1, source_target_pairs={{0,3},{1,2},{2,1},{3,0},{4,7},{5,6},{6,5},{7,4},{8,11},{9,10},{10,... | collective-permute-start | bytes 9224 | tf_op jit(solution)/shard_map/ppermute | solution.py:227
  47.9 4.5 %collective-permute-done.5 = bf16[96,768]{1,0:T(8,128)(2,1)} collective-permute-done((bf16[96,768]{1,0:T(8,128)(2,1)}, bf16[96,768]{1,0:T(8,128)(2,1)}, u32[]{:S(2)}, u32[]{:S(2)}) %collective-permute-start.5) | collective-permute-done | bytes 147488 | tf_op jit(solution)/shard_map/ppermute | solution.py:227
  52.4 1.0 pad_maximum_fusion.6.refs_0_
  53.5 1.5 %collective-permute-start.8 = (bf16[2,96,768]{2,1,0:T(8,128)(2,1)S(1)}, bf16[2,96,768]{2,1,0:T(8,128)(2,1)S(1)}, u32[]{:S(2)}, u32[]{:S(2)}) collective-permute-start(bf16[2,96,768]{2,1,0:T(8,128)(2,1)S(1)} %pad_maximum_fusion.6.refs_0_), channel_id=1, source_target_pairs={{0,8},{4,12},{8,0},{12,4},{16,24},{20,28},{24,16},{28,20},{1,9},{5... | collective-permute-start | bytes 884744 | tf_op jit(solution)/shard_map/ppermute | solution.py:224
  55.0 2.4 %collective-permute-start.10 = (bf16[2,96,768]{2,1,0:T(8,128)(2,1)S(1)}, bf16[2,96,768]{2,1,0:T(8,128)(2,1)S(1)}, u32[]{:S(2)}, u32[]{:S(2)}) collective-permute-start(bf16[2,96,768]{2,1,0:T(8,128)(2,1)S(1)} %pad_maximum_fusion.6.refs_0_), channel_id=1, source_target_pairs={{0,16},{4,20},{8,24},{12,28},{16,0},{20,4},{24,8},{28,12},{1,17},{... | collective-permute-start | bytes 884744 | tf_op jit(solution)/shard_map/ppermute | solution.py:224
  57.5 7.4 %shard_map.102 = (bf16[4,1280,192]{2,1,0:T(8,128)(2,1)S(1)}, bf16[768,768]{1,0:T(8,128)(2,1)S(1)}) custom-call(s32[16]{0:T(128)S(1)} %copy-done.10, s32[2]{0:T(128)S(1)} %pad_add_fusion.meta_ref, bf16[1280,768]{1,0:T(8,128)(2,1)S(1)} %copy-done.3, bf16[1280,768]{1,0:T(8,128)(2,1)S(1)} %copy-done.6, bf16[384,768]{1,0:T(8,128)(2,1)} %collective-permute-done.refs_0_, ...), custom_call_target="tpu_custom_call" | custom-call | flops 4529848320 | bytes 7864320 | tf_op jit(solution)/shard_map/pallas_call | solution.py:301
  65.5 5.7 %collective-permute-done.10.refs_4_ = bf16[2,96,768]{2,1,0:T(8,128)(2,1)S(1)} collective-permute-done((bf16[2,96,768]{2,1,0:T(8,128)(2,1)S(1)}, bf16[2,96,768]{2,1,0:T(8,128)(2,1)S(1)}, u32[]{:S(2)}, u32[]{:S(2)}) %collective-permute-start.10) | collective-permute-done | bytes 294944 | tf_op jit(solution)/shard_map/ppermute | solution.py:224
  71.9 1.3 %collective-permute-done.15 = f32[1,768]{1,0:T(1,128)S(1)} collective-permute-done((f32[1,768]{1,0:T(1,128)S(1)}, f32[1,768]{1,0:T(1,128)S(1)}, u32[]{:S(2)}, u32[]{:S(2)}) %collective-permute-start.15) | collective-permute-done | bytes 3104 | tf_op jit(solution)/shard_map/ppermute | solution.py:224
  73.3 1.1 %collective-permute-start.16 = (bf16[112,768]{1,0:T(8,128)(2,1)S(1)}, bf16[112,768]{1,0:T(8,128)(2,1)S(1)}, u32[]{:S(2)}, u32[]{:S(2)}) collective-permute-start(bf16[112,768]{1,0:T(8,128)(2,1)S(1)} %get-tuple-element.65), channel_id=1, source_target_pairs={{0,8},{4,12},{8,0},{12,4},{16,24},{20,28},{24,16},{28,20},{1,9},{5... | collective-permute-start | bytes 516104 | tf_op jit(solution)/shard_map/ppermute | solution.py:224
  74.4 1.1 %collective-permute-start.17 = (bf16[112,768]{1,0:T(8,128)(2,1)S(1)}, bf16[112,768]{1,0:T(8,128)(2,1)S(1)}, u32[]{:S(2)}, u32[]{:S(2)}) collective-permute-start(bf16[112,768]{1,0:T(8,128)(2,1)S(1)} %get-tuple-element.64), channel_id=1, source_target_pairs={{0,16},{4,20},{8,24},{12,28},{16,0},{20,4},{24,8},{28,12},{1,17},{... | collective-permute-start | bytes 516104 | tf_op jit(solution)/shard_map/ppermute | solution.py:224
  75.5 1.4 %collective-permute-start.18 = (bf16[112,768]{1,0:T(8,128)(2,1)S(1)}, bf16[112,768]{1,0:T(8,128)(2,1)S(1)}, u32[]{:S(2)}, u32[]{:S(2)}) collective-permute-start(bf16[112,768]{1,0:T(8,128)(2,1)S(1)} %get-tuple-element.63), channel_id=1, source_target_pairs={{0,24},{4,28},{8,16},{12,20},{16,8},{20,12},{24,0},{28,4},{1,25},{... | collective-permute-start | bytes 516104 | tf_op jit(solution)/shard_map/ppermute | solution.py:224
  76.9 26.5 %shard_map.103 = (bf16[1280,768]{1,0:T(8,128)(2,1)}, bf16[1280,768]{1,0:T(8,128)(2,1)}) custom-call(s32[16]{0:T(128)S(1)} %copy-done.10, s32[2]{0:T(128)S(1)} %pad_add_fusion.meta_ref, bf16[1280,768]{1,0:T(8,128)(2,1)S(1)} %bitcast.49, bf16[1280,768]{1,0:T(8,128)(2,1)S(1)} %copy-done.3, bf16[1280,768]{1,0:T(8,128)(2,1)S(1)} %copy-done.6, ...), custom_call_target="tpu_custom_call" | custom-call | flops 15099494400 | bytes 7864320 | tf_op jit(solution)/shard_map/pallas_call | solution.py:322
  (60 shorter events, 6.2 us)
Async XLA Ops:
  2.0 16.5 %collective-permute-start = (bf16[384,768]{1,0:T(8,128)(2,1)S(1)}, bf16[384,768]{1,0:T(8,128)(2,1)}, u32[]{:S(2)}, u32[]{:S(2)}) collective-permute-start(bf16[384,768]{1,0:T(8,128)(2,1)S(1)} %fusion), channel_id=1, source_target_pairs={{0,1},{1,0},{2,3},{3,2},{4,5},{5,4},{6,7},{7,6},{8,9},{9,8},{10,11... | collective-permute-start | bytes 1769480 | tf_op jit(solution)/shard_map/ppermute | solution.py:227
  18.6 38.9 %collective-permute-start.1 = (bf16[384,768]{1,0:T(8,128)(2,1)}, bf16[384,768]{1,0:T(8,128)(2,1)}, u32[]{:S(2)}, u32[]{:S(2)}) collective-permute-start(bf16[384,768]{1,0:T(8,128)(2,1)} %collective-permute-done.refs_0_), channel_id=1, source_target_pairs={{0,4},{4,0},{8,12},{12,8},{16,20},{20,16},{24,28},{28,24},{1,5},{5... | collective-permute-start | bytes 1769480 | tf_op jit(solution)/shard_map/ppermute | solution.py:224
  19.2 17.0 %copy-start = (bf16[768,3,3,64]{0,3,2,1:T(8,128)(2,1)S(1)}, bf16[768,3,3,64]{0,3,2,1:T(8,128)(2,1)}, u32[]{:S(2)}) copy-start(bf16[768,3,3,64]{0,3,2,1:T(8,128)(2,1)} %param.9) | copy-start | bytes 2654212
  31.9 21.6 %collective-permute-start.2 = (f32[1,768]{1,0:T(1,128)S(1)}, f32[1,768]{1,0:T(1,128)S(1)}, u32[]{:S(2)}, u32[]{:S(2)}) collective-permute-start(f32[1,768]{1,0:T(1,128)S(1)} %get-tuple-element.30), channel_id=1, source_target_pairs={{0,1},{1,0},{2,3},{3,2},{4,5},{5,4},{6,7},{7,6},{8,9},{9,8},{10,11... | collective-permute-start | bytes 9224 | tf_op jit(solution)/shard_map/ppermute | solution.py:227
  33.6 21.4 %collective-permute-start.3 = (f32[1,768]{1,0:T(1,128)S(1)}, f32[1,768]{1,0:T(1,128)S(1)}, u32[]{:S(2)}, u32[]{:S(2)}) collective-permute-start(f32[1,768]{1,0:T(1,128)S(1)} %get-tuple-element.30), channel_id=1, source_target_pairs={{0,2},{1,3},{2,0},{3,1},{4,6},{5,7},{6,4},{7,5},{8,10},{9,11},{10,... | collective-permute-start | bytes 9224 | tf_op jit(solution)/shard_map/ppermute | solution.py:227
  36.9 9.0 %collective-permute-start.6 = (bf16[96,768]{1,0:T(8,128)(2,1)}, bf16[96,768]{1,0:T(8,128)(2,1)}, u32[]{:S(2)}, u32[]{:S(2)}) collective-permute-start(bf16[96,768]{1,0:T(8,128)(2,1)} %fusion.11), channel_id=1, source_target_pairs={{0,3},{1,2},{2,1},{3,0},{4,7},{5,6},{6,5},{7,4},{8,11},{9,10},{10,... | collective-permute-start | bytes 442376 | tf_op jit(solution)/shard_map/ppermute | solution.py:227
  37.0 15.4 %collective-permute-start.5 = (bf16[96,768]{1,0:T(8,128)(2,1)}, bf16[96,768]{1,0:T(8,128)(2,1)}, u32[]{:S(2)}, u32[]{:S(2)}) collective-permute-start(bf16[96,768]{1,0:T(8,128)(2,1)} %fusion.11), channel_id=1, source_target_pairs={{0,2},{1,3},{2,0},{3,1},{4,6},{5,7},{6,4},{7,5},{8,10},{9,11},{10,... | collective-permute-start | bytes 442376 | tf_op jit(solution)/shard_map/ppermute | solution.py:227
  42.1 15.3 %copy-start.3 = (bf16[1280,768]{1,0:T(8,128)(2,1)S(1)}, bf16[1280,768]{1,0:T(8,128)(2,1)}, u32[]{:S(2)}) copy-start(bf16[1280,768]{1,0:T(8,128)(2,1)} %copy-done.1) | copy-start | bytes 5898244
  42.1 15.3 %copy-start.6 = (bf16[1280,768]{1,0:T(8,128)(2,1)S(1)}, bf16[1280,768]{1,0:T(8,128)(2,1)}, u32[]{:S(2)}) copy-start(bf16[1280,768]{1,0:T(8,128)(2,1)} %copy-done.4) | copy-start | bytes 5898244
  42.1 15.3 %copy-start.10 = (s32[16]{0:T(128)S(1)}, s32[16]{0:T(128)}, u32[]{:S(2)}) copy-start(s32[16]{0:T(128)} %len_ref.5) | copy-start | bytes 196
  46.0 18.9 %collective-permute-start.4 = (f32[1,768]{1,0:T(1,128)S(1)}, f32[1,768]{1,0:T(1,128)S(1)}, u32[]{:S(2)}, u32[]{:S(2)}) collective-permute-start(f32[1,768]{1,0:T(1,128)S(1)} %get-tuple-element.30), channel_id=1, source_target_pairs={{0,3},{1,2},{2,1},{3,0},{4,7},{5,6},{6,5},{7,4},{8,11},{9,10},{10,... | collective-permute-start | bytes 9224 | tf_op jit(solution)/shard_map/ppermute | solution.py:227
  52.4 19.3 %collective-permute-start.14 = (bf16[4,96,768]{2,1,0:T(8,128)(2,1)S(1)}, bf16[4,96,768]{2,1,0:T(8,128)(2,1)S(1)}, u32[]{:S(2)}, u32[]{:S(2)}) collective-permute-start(bf16[4,96,768]{2,1,0:T(8,128)(2,1)S(1)} %get-tuple-element.35), channel_id=1, source_target_pairs={{0,4},{4,0},{8,12},{12,8},{16,20},{20,16},{24,28},{28,24},{1,5},{5... | collective-permute-start | bytes 1769480 | tf_op jit(solution)/shard_map/ppermute | solution.py:224
  53.5 11.5 %collective-permute-start.8 = (bf16[2,96,768]{2,1,0:T(8,128)(2,1)S(1)}, bf16[2,96,768]{2,1,0:T(8,128)(2,1)S(1)}, u32[]{:S(2)}, u32[]{:S(2)}) collective-permute-start(bf16[2,96,768]{2,1,0:T(8,128)(2,1)S(1)} %pad_maximum_fusion.6.refs_0_), channel_id=1, source_target_pairs={{0,8},{4,12},{8,0},{12,4},{16,24},{20,28},{24,16},{28,20},{1,9},{5... | collective-permute-start | bytes 884744 | tf_op jit(solution)/shard_map/ppermute | solution.py:224
  55.0 16.1 %collective-permute-start.10 = (bf16[2,96,768]{2,1,0:T(8,128)(2,1)S(1)}, bf16[2,96,768]{2,1,0:T(8,128)(2,1)S(1)}, u32[]{:S(2)}, u32[]{:S(2)}) collective-permute-start(bf16[2,96,768]{2,1,0:T(8,128)(2,1)S(1)} %pad_maximum_fusion.6.refs_0_), channel_id=1, source_target_pairs={{0,16},{4,20},{8,24},{12,28},{16,0},{20,4},{24,8},{28,12},{1,17},{... | collective-permute-start | bytes 884744 | tf_op jit(solution)/shard_map/ppermute | solution.py:224
  57.4 13.7 %collective-permute-start.12 = (bf16[2,96,768]{2,1,0:T(8,128)(2,1)S(1)}, bf16[2,96,768]{2,1,0:T(8,128)(2,1)S(1)}, u32[]{:S(2)}, u32[]{:S(2)}) collective-permute-start(bf16[2,96,768]{2,1,0:T(8,128)(2,1)S(1)} %pad_maximum_fusion.6.refs_0_), channel_id=1, source_target_pairs={{0,24},{4,28},{8,16},{12,20},{16,8},{20,12},{24,0},{28,4},{1,25},{... | collective-permute-start | bytes 884744 | tf_op jit(solution)/shard_map/ppermute | solution.py:224
  64.8 12.1 %copy-start.7 = (bf16[3,64,768]{2,1,0:T(8,128)(2,1)S(1)}, bf16[3,64,768]{2,1,0:T(8,128)(2,1)}, u32[]{:S(2)}) copy-start(bf16[3,64,768]{2,1,0:T(8,128)(2,1)} %param.10) | copy-start | bytes 884740
  64.9 9.6 %collective-permute-start.7 = (bf16[2,96,768]{2,1,0:T(8,128)(2,1)S(1)}, bf16[2,96,768]{2,1,0:T(8,128)(2,1)S(1)}, u32[]{:S(2)}, u32[]{:S(2)}) collective-permute-start(bf16[2,96,768]{2,1,0:T(8,128)(2,1)S(1)} %pad_maximum_fusion.6.refs_0_), channel_id=1, source_target_pairs={{0,4},{4,0},{8,12},{12,8},{16,20},{20,16},{24,28},{28,24},{1,5},{5... | collective-permute-start | bytes 884744 | tf_op jit(solution)/shard_map/ppermute | solution.py:224
  65.0 10.5 %collective-permute-start.9 = (bf16[2,96,768]{2,1,0:T(8,128)(2,1)S(1)}, bf16[2,96,768]{2,1,0:T(8,128)(2,1)S(1)}, u32[]{:S(2)}, u32[]{:S(2)}) collective-permute-start(bf16[2,96,768]{2,1,0:T(8,128)(2,1)S(1)} %collective-permute-done.8.refs_2_), channel_id=1, source_target_pairs={{0,4},{4,0},{8,12},{12,8},{16,20},{20,16},{24,28},{28,24},{1,5},{5... | collective-permute-start | bytes 884744 | tf_op jit(solution)/shard_map/ppermute | solution.py:224
  71.2 5.7 %collective-permute-start.11 = (bf16[2,96,768]{2,1,0:T(8,128)(2,1)S(1)}, bf16[2,96,768]{2,1,0:T(8,128)(2,1)S(1)}, u32[]{:S(2)}, u32[]{:S(2)}) collective-permute-start(bf16[2,96,768]{2,1,0:T(8,128)(2,1)S(1)} %collective-permute-done.10.refs_4_), channel_id=1, source_target_pairs={{0,4},{4,0},{8,12},{12,8},{16,20},{20,16},{24,28},{28,24},{1,5},{5... | collective-permute-start | bytes 884744 | tf_op jit(solution)/shard_map/ppermute | solution.py:224
  71.2 5.7 %collective-permute-start.13 = (bf16[2,96,768]{2,1,0:T(8,128)(2,1)S(1)}, bf16[2,96,768]{2,1,0:T(8,128)(2,1)S(1)}, u32[]{:S(2)}, u32[]{:S(2)}) collective-permute-start(bf16[2,96,768]{2,1,0:T(8,128)(2,1)S(1)} %collective-permute-done.12.refs_6_), channel_id=1, source_target_pairs={{0,4},{4,0},{8,12},{12,8},{16,20},{20,16},{24,28},{28,24},{1,5},{5... | collective-permute-start | bytes 884744 | tf_op jit(solution)/shard_map/ppermute | solution.py:224
  71.7 1.5 %collective-permute-start.15 = (f32[1,768]{1,0:T(1,128)S(1)}, f32[1,768]{1,0:T(1,128)S(1)}, u32[]{:S(2)}, u32[]{:S(2)}) collective-permute-start(f32[1,768]{1,0:T(1,128)S(1)} %add_add_fusion), channel_id=1, source_target_pairs={{0,4},{4,0},{8,12},{12,8},{16,20},{20,16},{24,28},{28,24},{1,5},{5... | collective-permute-start | bytes 9224 | tf_op jit(solution)/shard_map/ppermute | solution.py:224
  73.3 30.1 %collective-permute-start.16 = (bf16[112,768]{1,0:T(8,128)(2,1)S(1)}, bf16[112,768]{1,0:T(8,128)(2,1)S(1)}, u32[]{:S(2)}, u32[]{:S(2)}) collective-permute-start(bf16[112,768]{1,0:T(8,128)(2,1)S(1)} %get-tuple-element.65), channel_id=1, source_target_pairs={{0,8},{4,12},{8,0},{12,4},{16,24},{20,28},{24,16},{28,20},{1,9},{5... | collective-permute-start | bytes 516104 | tf_op jit(solution)/shard_map/ppermute | solution.py:224
  74.4 29.0 %collective-permute-start.17 = (bf16[112,768]{1,0:T(8,128)(2,1)S(1)}, bf16[112,768]{1,0:T(8,128)(2,1)S(1)}, u32[]{:S(2)}, u32[]{:S(2)}) collective-permute-start(bf16[112,768]{1,0:T(8,128)(2,1)S(1)} %get-tuple-element.64), channel_id=1, source_target_pairs={{0,16},{4,20},{8,24},{12,28},{16,0},{20,4},{24,8},{28,12},{1,17},{... | collective-permute-start | bytes 516104 | tf_op jit(solution)/shard_map/ppermute | solution.py:224
  75.5 28.0 %collective-permute-start.18 = (bf16[112,768]{1,0:T(8,128)(2,1)S(1)}, bf16[112,768]{1,0:T(8,128)(2,1)S(1)}, u32[]{:S(2)}, u32[]{:S(2)}) collective-permute-start(bf16[112,768]{1,0:T(8,128)(2,1)S(1)} %get-tuple-element.63), channel_id=1, source_target_pairs={{0,24},{4,28},{8,16},{12,20},{16,8},{20,12},{24,0},{28,4},{1,25},{... | collective-permute-start | bytes 516104 | tf_op jit(solution)/shard_map/ppermute | solution.py:224
  (6 other events, 18.3 us)

commit v3 on v2

--- a/solution.py
+++ b/solution.py
@@ -286,7 +286,7 @@
         [row_of(big)] * 2 + [whole((1, d)), whole((3 * n, d)), whole((n, d))],
         [row_of(big)] * 2 + [all_of(big), whole((1, d))],
         [row_shape, row_shape, all_shape, jax.ShapeDtypeStruct((1, d), F32)], big_scratch,
-    )(hist_len, in_hbm(flat_states), in_hbm(flat_cot), gain, in_hbm(qkv_rows), in_hbm(wo_rows))
+    )(hist_len, in_hbm(flat_states), in_hbm(flat_cot), gain, qkv_rows, wo_rows)
 
     piece = (d // parts, 4 * n)
     half = parts // 2
@@ -297,7 +297,9 @@
         [jax.ShapeDtypeStruct(piece, F32)] * half + [jax.ShapeDtypeStruct((half,) + piece, BF16)],
         [pltpu.VMEM((4, parts, d // parts, n), F32)],
     )(meta, normed, mcot, all0)
-    others = [hop_mp(gain_part, k) for k in range(1, mp)]
+    others = []
+    for k in range(1, mp):
+        others.append(hop_mp(gain_part, k))
     all1, wt1 = call(
         functools.partial(far_kernel, seq, heads, width), 3 * flops_in, 28, 2, 2,
         [row_of(big)] * 2 + [any_spec] * 2,

time: 106 us -> 108 us (1.019)
  local copies, waits for them, and re-layouts: 8.81 us -> 10.9 us
    unnamed x22 -> x26, local copies, waits for them, and re-layouts: 6.31 us -> 8.44 us
  transfers between devices with their start and end apart: 19 -> 19, of which waited for: 4 -> 4; matrix products, arithmetic and copies ran while one was open for 3% -> 3% of each run, Pallas kernels for 45% -> 44%
where the time goes in v3:
time: 108 us
  Pallas kernels  47.3 us (44%)
  waiting for transfers between devices  24.2 us (22%)
  starting transfers between devices  20 us (19%)
  local copies, waits for them, and re-layouts  10.9 us (10%)
  other arithmetic  4.18 us (4%)
    pallas_call x1, Pallas kernels, body(): call(functools.partial(final_kernel, seq, heads, width, parts, mp), 10 *...  26.5 us
    ppermute x6, waiting for transfers between devices, hop_mp(): return lax.ppermute(x, 'mp', [(i, i ^ k) for i in range(mp)])  17.2 us
    ppermute x6, starting transfers between devices, hop_mp(): return lax.ppermute(x, 'mp', [(i, i ^ k) for i in range(mp)])  11.3 us
    pallas_call x1, Pallas kernels, body(): call(functools.partial(own_kernel, seq, heads, width), 3 * flops_in, 28,...  9.53 us
    ppermute x13, starting transfers between devices, hop_dp(): return lax.ppermute(x, 'dp', [(i, i ^ r * low) for i in range(dp)])  8.69 us
    unnamed x26, local copies, waits for them, and re-layouts  8.44 us
    pallas_call x1, Pallas kernels, body(): call(functools.partial(far_kernel, seq, heads, width), 3 * flops_in, 28,...  7.38 us
    ppermute x13, waiting for transfers between devices, hop_dp(): return lax.ppermute(x, 'dp', [(i, i ^ r * low) for i in range(dp)])  7 us
  transfers between devices with their start and end apart: 19, of which 4 were waited for; matrix products, arithmetic and copies ran while one was open for 3% of the time, Pallas kernels for 44%

profile of v3, /device:TPU:0, one launch (start us, length us, event | category | flops | bytes accessed | tf_op | source)
XLA Modules:
  0.0 107.5 jit_solution(12182577611899878297)
XLA Ops:
  0.6 1.4 %fusion = bf16[384,768]{1,0:T(8,128)(2,1)S(1)} fusion(s32[]{:T(128)S(6)} %select_n.17, bf16[576,768]{1,0:T(8,128)(2,1)} %bitcast.40, bf16[192,768]{1,0:T(8,128)(2,1)} %bitcast.44), kind=kLoop, calls=%fused_computation.4 | loop fusion | flops 1179648 | bytes 1769476 | tf_op jit(solution)/shard_map/concatenate | solution.py:232
  2.0 3.1 %collective-permute-start = (bf16[384,768]{1,0:T(8,128)(2,1)S(1)}, bf16[384,768]{1,0:T(8,128)(2,1)}, u32[]{:S(2)}, u32[]{:S(2)}) collective-permute-start(bf16[384,768]{1,0:T(8,128)(2,1)S(1)} %fusion), channel_id=1, source_target_pairs={{0,1},{1,0},{2,3},{3,2},{4,5},{5,4},{6,7},{7,6},{8,9},{9,8},{10,11... | collective-permute-start | bytes 1769480 | tf_op jit(solution)/shard_map/ppermute | solution.py:227
  5.8 12.7 %collective-permute-done.refs_0_ = bf16[384,768]{1,0:T(8,128)(2,1)} collective-permute-done((bf16[384,768]{1,0:T(8,128)(2,1)S(1)}, bf16[384,768]{1,0:T(8,128)(2,1)}, u32[]{:S(2)}, u32[]{:S(2)}) %collective-permute-start) | collective-permute-done | bytes 589856 | tf_op jit(solution)/shard_map/ppermute | solution.py:227
  18.6 1.2 %copy-done = bf16[768,3,3,64]{0,3,2,1:T(8,128)(2,1)S(1)} copy-done((bf16[768,3,3,64]{0,3,2,1:T(8,128)(2,1)S(1)}, bf16[768,3,3,64]{0,3,2,1:T(8,128)(2,1)}, u32[]{:S(2)}) %copy-start) | copy-done | bytes 884760
  21.4 9.5 %shard_map.101 = (bf16[1280,768]{1,0:T(8,128)(2,1)S(1)}, bf16[1280,768]{1,0:T(8,128)(2,1)S(1)}, bf16[4,1280,192]{2,1,0:T(8,128)(2,1)S(1)}, f32[1,768]{1,0:T(1,128)S(1)}) custom-call(s32[16]{0:T(128)S(1)} %copy-done.11, bf16[1280,768]{1,0:T(8,128)(2,1)} %bitcast.48, bf16[1280,768]{1,0:T(8,128)(2,1)} %bitcast.52, f32[1,768]{1,0:T(1,128)S(1)} %reshape.49.gain_ref, ...), custom_call_target="tpu_custom_call" | custom-call | flops 4529848320 | bytes 7864320 | tf_op jit(solution)/shard_map/pallas_call | solution.py:284
  30.9 1.3 %copy-done.2 = bf16[1280,768]{1,0:T(8,128)(2,1)} copy-done((bf16[1280,768]{1,0:T(8,128)(2,1)}, bf16[1280,768]{1,0:T(8,128)(2,1)S(1)}, u32[]{:S(2)}) %copy-start.2) | copy-done | bytes 1966104
  32.2 1.3 %copy-done.5 = bf16[1280,768]{1,0:T(8,128)(2,1)} copy-done((bf16[1280,768]{1,0:T(8,128)(2,1)}, bf16[1280,768]{1,0:T(8,128)(2,1)S(1)}, u32[]{:S(2)}) %copy-start.5) | copy-done | bytes 1966104
  33.4 1.7 %collective-permute-start.2 = (f32[1,768]{1,0:T(1,128)S(1)}, f32[1,768]{1,0:T(1,128)S(1)}, u32[]{:S(2)}, u32[]{:S(2)}) collective-permute-start(f32[1,768]{1,0:T(1,128)S(1)} %get-tuple-element.30), channel_id=1, source_target_pairs={{0,1},{1,0},{2,3},{3,2},{4,5},{5,4},{6,7},{7,6},{8,9},{9,8},{10,11... | collective-permute-start | bytes 9224 | tf_op jit(solution)/shard_map/ppermute | solution.py:227
  35.2 2.6 %collective-permute-start.3 = (f32[1,768]{1,0:T(1,128)S(1)}, f32[1,768]{1,0:T(1,128)S(1)}, u32[]{:S(2)}, u32[]{:S(2)}) collective-permute-start(f32[1,768]{1,0:T(1,128)S(1)} %get-tuple-element.30), channel_id=1, source_target_pairs={{0,2},{1,3},{2,0},{3,1},{4,6},{5,7},{6,4},{7,5},{8,10},{9,11},{10,... | collective-permute-start | bytes 9224 | tf_op jit(solution)/shard_map/ppermute | solution.py:227
  38.6 1.9 %collective-permute-start.5 = (bf16[96,768]{1,0:T(8,128)(2,1)}, bf16[96,768]{1,0:T(8,128)(2,1)}, u32[]{:S(2)}, u32[]{:S(2)}) collective-permute-start(bf16[96,768]{1,0:T(8,128)(2,1)} %fusion.11), channel_id=1, source_target_pairs={{0,2},{1,3},{2,0},{3,1},{4,6},{5,7},{6,4},{7,5},{8,10},{9,11},{10,... | collective-permute-start | bytes 442376 | tf_op jit(solution)/shard_map/ppermute | solution.py:227
  40.6 1.5 %copy-done.3 = bf16[1280,768]{1,0:T(8,128)(2,1)S(1)} copy-done((bf16[1280,768]{1,0:T(8,128)(2,1)S(1)}, bf16[1280,768]{1,0:T(8,128)(2,1)}, u32[]{:S(2)}) %copy-start.3) | copy-done | bytes 1966104
  42.1 1.5 %copy-done.6 = bf16[1280,768]{1,0:T(8,128)(2,1)S(1)} copy-done((bf16[1280,768]{1,0:T(8,128)(2,1)S(1)}, bf16[1280,768]{1,0:T(8,128)(2,1)}, u32[]{:S(2)}) %copy-start.6) | copy-done | bytes 1966104
  43.7 3.8 %shard_map.104 = (f32[96,768]{1,0:T(8,128)S(1)}, f32[96,768]{1,0:T(8,128)S(1)}, f32[96,768]{1,0:T(8,128)S(1)}, f32[96,768]{1,0:T(8,128)S(1)}, bf16[4,96,768]{2,1,0:T(8,128)(2,1)S(1)}) custom-call(s32[2]{0:T(128)S(1)} %pad_add_fusion.meta_ref, bf16[1280,768]{1,0:T(8,128)(2,1)S(1)} %copy-done.3, bf16[1280,768]{1,0:T(8,128)(2,1)S(1)} %copy-done.6, ...), custom_call_target="tpu_custom_call" | custom-call | flops 1509949440 | bytes 7864320 | tf_op jit(solution)/shard_map/pallas_call | solution.py:293
  47.5 2.0 %collective-permute-start.4 = (f32[1,768]{1,0:T(1,128)S(1)}, f32[1,768]{1,0:T(1,128)S(1)}, u32[]{:S(2)}, u32[]{:S(2)}) collective-permute-start(f32[1,768]{1,0:T(1,128)S(1)} %get-tuple-element.30), channel_id=1, source_target_pairs={{0,3},{1,2},{2,1},{3,0},{4,7},{5,6},{6,5},{7,4},{8,11},{9,10},{10,... | collective-permute-start | bytes 9224 | tf_op jit(solution)/shard_map/ppermute | solution.py:227
  49.5 4.5 %collective-permute-done.5 = bf16[96,768]{1,0:T(8,128)(2,1)} collective-permute-done((bf16[96,768]{1,0:T(8,128)(2,1)}, bf16[96,768]{1,0:T(8,128)(2,1)}, u32[]{:S(2)}, u32[]{:S(2)}) %collective-permute-start.5) | collective-permute-done | bytes 147488 | tf_op jit(solution)/shard_map/ppermute | solution.py:227
  55.0 1.6 %collective-permute-start.8 = (bf16[2,96,768]{2,1,0:T(8,128)(2,1)S(1)}, bf16[2,96,768]{2,1,0:T(8,128)(2,1)S(1)}, u32[]{:S(2)}, u32[]{:S(2)}) collective-permute-start(bf16[2,96,768]{2,1,0:T(8,128)(2,1)S(1)} %pad_maximum_fusion.6.refs_0_), channel_id=1, source_target_pairs={{0,8},{4,12},{8,0},{12,4},{16,24},{20,28},{24,16},{28,20},{1,9},{5... | collective-permute-start | bytes 884744 | tf_op jit(solution)/shard_map/ppermute | solution.py:224
  56.6 2.4 %collective-permute-start.10 = (bf16[2,96,768]{2,1,0:T(8,128)(2,1)S(1)}, bf16[2,96,768]{2,1,0:T(8,128)(2,1)S(1)}, u32[]{:S(2)}, u32[]{:S(2)}) collective-permute-start(bf16[2,96,768]{2,1,0:T(8,128)(2,1)S(1)} %pad_maximum_fusion.6.refs_0_), channel_id=1, source_target_pairs={{0,16},{4,20},{8,24},{12,28},{16,0},{20,4},{24,8},{28,12},{1,17},{... | collective-permute-start | bytes 884744 | tf_op jit(solution)/shard_map/ppermute | solution.py:224
  59.0 7.4 %shard_map.102 = (bf16[4,1280,192]{2,1,0:T(8,128)(2,1)S(1)}, bf16[768,768]{1,0:T(8,128)(2,1)S(1)}) custom-call(s32[16]{0:T(128)S(1)} %copy-done.12, s32[2]{0:T(128)S(1)} %pad_add_fusion.meta_ref, bf16[1280,768]{1,0:T(8,128)(2,1)S(1)} %copy-done.4, bf16[1280,768]{1,0:T(8,128)(2,1)S(1)} %copy-done.7, bf16[384,768]{1,0:T(8,128)(2,1)} %collective-permute-done.refs_0_, ...), custom_call_target="tpu_custom_call" | custom-call | flops 4529848320 | bytes 7864320 | tf_op jit(solution)/shard_map/pallas_call | solution.py:303
  67.0 5.7 %collective-permute-done.10.refs_4_ = bf16[2,96,768]{2,1,0:T(8,128)(2,1)S(1)} collective-permute-done((bf16[2,96,768]{2,1,0:T(8,128)(2,1)S(1)}, bf16[2,96,768]{2,1,0:T(8,128)(2,1)S(1)}, u32[]{:S(2)}, u32[]{:S(2)}) %collective-permute-start.10) | collective-permute-done | bytes 294944 | tf_op jit(solution)/shard_map/ppermute | solution.py:224
  73.4 1.3 %collective-permute-done.15 = f32[1,768]{1,0:T(1,128)S(1)} collective-permute-done((f32[1,768]{1,0:T(1,128)S(1)}, f32[1,768]{1,0:T(1,128)S(1)}, u32[]{:S(2)}, u32[]{:S(2)}) %collective-permute-start.15) | collective-permute-done | bytes 3104 | tf_op jit(solution)/shard_map/ppermute | solution.py:224
  74.9 1.1 %collective-permute-start.16 = (bf16[112,768]{1,0:T(8,128)(2,1)S(1)}, bf16[112,768]{1,0:T(8,128)(2,1)S(1)}, u32[]{:S(2)}, u32[]{:S(2)}) collective-permute-start(bf16[112,768]{1,0:T(8,128)(2,1)S(1)} %get-tuple-element.65), channel_id=1, source_target_pairs={{0,8},{4,12},{8,0},{12,4},{16,24},{20,28},{24,16},{28,20},{1,9},{5... | collective-permute-start | bytes 516104 | tf_op jit(solution)/shard_map/ppermute | solution.py:224
  76.0 1.1 %collective-permute-start.17 = (bf16[112,768]{1,0:T(8,128)(2,1)S(1)}, bf16[112,768]{1,0:T(8,128)(2,1)S(1)}, u32[]{:S(2)}, u32[]{:S(2)}) collective-permute-start(bf16[112,768]{1,0:T(8,128)(2,1)S(1)} %get-tuple-element.64), channel_id=1, source_target_pairs={{0,16},{4,20},{8,24},{12,28},{16,0},{20,4},{24,8},{28,12},{1,17},{... | collective-permute-start | bytes 516104 | tf_op jit(solution)/shard_map/ppermute | solution.py:224
  77.1 1.4 %collective-permute-start.18 = (bf16[112,768]{1,0:T(8,128)(2,1)S(1)}, bf16[112,768]{1,0:T(8,128)(2,1)S(1)}, u32[]{:S(2)}, u32[]{:S(2)}) collective-permute-start(bf16[112,768]{1,0:T(8,128)(2,1)S(1)} %get-tuple-element.63), channel_id=1, source_target_pairs={{0,24},{4,28},{8,16},{12,20},{16,8},{20,12},{24,0},{28,4},{1,25},{... | collective-permute-start | bytes 516104 | tf_op jit(solution)/shard_map/ppermute | solution.py:224
  78.5 26.5 %shard_map.103 = (bf16[1280,768]{1,0:T(8,128)(2,1)}, bf16[1280,768]{1,0:T(8,128)(2,1)}) custom-call(s32[16]{0:T(128)S(1)} %copy-done.12, s32[2]{0:T(128)S(1)} %pad_add_fusion.meta_ref, bf16[1280,768]{1,0:T(8,128)(2,1)S(1)} %bitcast.49, bf16[1280,768]{1,0:T(8,128)(2,1)S(1)} %copy-done.4, bf16[1280,768]{1,0:T(8,128)(2,1)S(1)} %copy-done.7, ...), custom_call_target="tpu_custom_call" | custom-call | flops 15099494400 | bytes 7864320 | tf_op jit(solution)/shard_map/pallas_call | solution.py:324
  (64 shorter events, 8.2 us)
Async XLA Ops:
  2.0 16.5 %collective-permute-start = (bf16[384,768]{1,0:T(8,128)(2,1)S(1)}, bf16[384,768]{1,0:T(8,128)(2,1)}, u32[]{:S(2)}, u32[]{:S(2)}) collective-permute-start(bf16[384,768]{1,0:T(8,128)(2,1)S(1)} %fusion), channel_id=1, source_target_pairs={{0,1},{1,0},{2,3},{3,2},{4,5},{5,4},{6,7},{7,6},{8,9},{9,8},{10,11... | collective-permute-start | bytes 1769480 | tf_op jit(solution)/shard_map/ppermute | solution.py:227
  18.6 40.4 %collective-permute-start.1 = (bf16[384,768]{1,0:T(8,128)(2,1)}, bf16[384,768]{1,0:T(8,128)(2,1)}, u32[]{:S(2)}, u32[]{:S(2)}) collective-permute-start(bf16[384,768]{1,0:T(8,128)(2,1)} %collective-permute-done.refs_0_), channel_id=1, source_target_pairs={{0,4},{4,0},{8,12},{12,8},{16,20},{20,16},{24,28},{28,24},{1,5},{5... | collective-permute-start | bytes 1769480 | tf_op jit(solution)/shard_map/ppermute | solution.py:224
  21.4 16.4 %copy-start.1 = (bf16[768,3,3,64]{0,3,2,1:T(8,128)(2,1)S(1)}, bf16[768,3,3,64]{0,3,2,1:T(8,128)(2,1)}, u32[]{:S(2)}) copy-start(bf16[768,3,3,64]{0,3,2,1:T(8,128)(2,1)} %param.9) | copy-start | bytes 2654212
  33.4 21.6 %collective-permute-start.2 = (f32[1,768]{1,0:T(1,128)S(1)}, f32[1,768]{1,0:T(1,128)S(1)}, u32[]{:S(2)}, u32[]{:S(2)}) collective-permute-start(f32[1,768]{1,0:T(1,128)S(1)} %get-tuple-element.30), channel_id=1, source_target_pairs={{0,1},{1,0},{2,3},{3,2},{4,5},{5,4},{6,7},{7,6},{8,9},{9,8},{10,11... | collective-permute-start | bytes 9224 | tf_op jit(solution)/shard_map/ppermute | solution.py:227
  35.2 21.4 %collective-permute-start.3 = (f32[1,768]{1,0:T(1,128)S(1)}, f32[1,768]{1,0:T(1,128)S(1)}, u32[]{:S(2)}, u32[]{:S(2)}) collective-permute-start(f32[1,768]{1,0:T(1,128)S(1)} %get-tuple-element.30), channel_id=1, source_target_pairs={{0,2},{1,3},{2,0},{3,1},{4,6},{5,7},{6,4},{7,5},{8,10},{9,11},{10,... | collective-permute-start | bytes 9224 | tf_op jit(solution)/shard_map/ppermute | solution.py:227
  38.5 9.0 %collective-permute-start.6 = (bf16[96,768]{1,0:T(8,128)(2,1)}, bf16[96,768]{1,0:T(8,128)(2,1)}, u32[]{:S(2)}, u32[]{:S(2)}) collective-permute-start(bf16[96,768]{1,0:T(8,128)(2,1)} %fusion.11), channel_id=1, source_target_pairs={{0,3},{1,2},{2,1},{3,0},{4,7},{5,6},{6,5},{7,4},{8,11},{9,10},{10,... | collective-permute-start | bytes 442376 | tf_op jit(solution)/shard_map/ppermute | solution.py:227
  38.6 15.4 %collective-permute-start.5 = (bf16[96,768]{1,0:T(8,128)(2,1)}, bf16[96,768]{1,0:T(8,128)(2,1)}, u32[]{:S(2)}, u32[]{:S(2)}) collective-permute-start(bf16[96,768]{1,0:T(8,128)(2,1)} %fusion.11), channel_id=1, source_target_pairs={{0,2},{1,3},{2,0},{3,1},{4,6},{5,7},{6,4},{7,5},{8,10},{9,11},{10,... | collective-permute-start | bytes 442376 | tf_op jit(solution)/shard_map/ppermute | solution.py:227
  43.7 15.3 %copy-start.4 = (bf16[1280,768]{1,0:T(8,128)(2,1)S(1)}, bf16[1280,768]{1,0:T(8,128)(2,1)}, u32[]{:S(2)}) copy-start(bf16[1280,768]{1,0:T(8,128)(2,1)} %copy-done.2) | copy-start | bytes 5898244
  43.7 15.3 %copy-start.7 = (bf16[1280,768]{1,0:T(8,128)(2,1)S(1)}, bf16[1280,768]{1,0:T(8,128)(2,1)}, u32[]{:S(2)}) copy-start(bf16[1280,768]{1,0:T(8,128)(2,1)} %copy-done.5) | copy-start | bytes 5898244
  43.7 15.4 %copy-start.12 = (s32[16]{0:T(128)S(1)}, s32[16]{0:T(128)}, u32[]{:S(2)}) copy-start(s32[16]{0:T(128)} %len_ref.5) | copy-start | bytes 196
  47.5 18.9 %collective-permute-start.4 = (f32[1,768]{1,0:T(1,128)S(1)}, f32[1,768]{1,0:T(1,128)S(1)}, u32[]{:S(2)}, u32[]{:S(2)}) collective-permute-start(f32[1,768]{1,0:T(1,128)S(1)} %get-tuple-element.30), channel_id=1, source_target_pairs={{0,3},{1,2},{2,1},{3,0},{4,7},{5,6},{6,5},{7,4},{8,11},{9,10},{10,... | collective-permute-start | bytes 9224 | tf_op jit(solution)/shard_map/ppermute | solution.py:227
  54.0 19.3 %collective-permute-start.14 = (bf16[4,96,768]{2,1,0:T(8,128)(2,1)S(1)}, bf16[4,96,768]{2,1,0:T(8,128)(2,1)S(1)}, u32[]{:S(2)}, u32[]{:S(2)}) collective-permute-start(bf16[4,96,768]{2,1,0:T(8,128)(2,1)S(1)} %get-tuple-element.35), channel_id=1, source_target_pairs={{0,4},{4,0},{8,12},{12,8},{16,20},{20,16},{24,28},{28,24},{1,5},{5... | collective-permute-start | bytes 1769480 | tf_op jit(solution)/shard_map/ppermute | solution.py:224
  55.0 11.5 %collective-permute-start.8 = (bf16[2,96,768]{2,1,0:T(8,128)(2,1)S(1)}, bf16[2,96,768]{2,1,0:T(8,128)(2,1)S(1)}, u32[]{:S(2)}, u32[]{:S(2)}) collective-permute-start(bf16[2,96,768]{2,1,0:T(8,128)(2,1)S(1)} %pad_maximum_fusion.6.refs_0_), channel_id=1, source_target_pairs={{0,8},{4,12},{8,0},{12,4},{16,24},{20,28},{24,16},{28,20},{1,9},{5... | collective-permute-start | bytes 884744 | tf_op jit(solution)/shard_map/ppermute | solution.py:224
  56.6 16.1 %collective-permute-start.10 = (bf16[2,96,768]{2,1,0:T(8,128)(2,1)S(1)}, bf16[2,96,768]{2,1,0:T(8,128)(2,1)S(1)}, u32[]{:S(2)}, u32[]{:S(2)}) collective-permute-start(bf16[2,96,768]{2,1,0:T(8,128)(2,1)S(1)} %pad_maximum_fusion.6.refs_0_), channel_id=1, source_target_pairs={{0,16},{4,20},{8,24},{12,28},{16,0},{20,4},{24,8},{28,12},{1,17},{... | collective-permute-start | bytes 884744 | tf_op jit(solution)/shard_map/ppermute | solution.py:224
  59.0 13.7 %collective-permute-start.12 = (bf16[2,96,768]{2,1,0:T(8,128)(2,1)S(1)}, bf16[2,96,768]{2,1,0:T(8,128)(2,1)S(1)}, u32[]{:S(2)}, u32[]{:S(2)}) collective-permute-start(bf16[2,96,768]{2,1,0:T(8,128)(2,1)S(1)} %pad_maximum_fusion.6.refs_0_), channel_id=1, source_target_pairs={{0,24},{4,28},{8,16},{12,20},{16,8},{20,12},{24,0},{28,4},{1,25},{... | collective-permute-start | bytes 884744 | tf_op jit(solution)/shard_map/ppermute | solution.py:224
  66.4 12.1 %copy-start.9 = (bf16[3,64,768]{2,1,0:T(8,128)(2,1)S(1)}, bf16[3,64,768]{2,1,0:T(8,128)(2,1)}, u32[]{:S(2)}) copy-start(bf16[3,64,768]{2,1,0:T(8,128)(2,1)} %param.10) | copy-start | bytes 884740
  66.5 9.6 %collective-permute-start.7 = (bf16[2,96,768]{2,1,0:T(8,128)(2,1)S(1)}, bf16[2,96,768]{2,1,0:T(8,128)(2,1)S(1)}, u32[]{:S(2)}, u32[]{:S(2)}) collective-permute-start(bf16[2,96,768]{2,1,0:T(8,128)(2,1)S(1)} %pad_maximum_fusion.6.refs_0_), channel_id=1, source_target_pairs={{0,4},{4,0},{8,12},{12,8},{16,20},{20,16},{24,28},{28,24},{1,5},{5... | collective-permute-start | bytes 884744 | tf_op jit(solution)/shard_map/ppermute | solution.py:224
  66.5 10.5 %collective-permute-start.9 = (bf16[2,96,768]{2,1,0:T(8,128)(2,1)S(1)}, bf16[2,96,768]{2,1,0:T(8,128)(2,1)S(1)}, u32[]{:S(2)}, u32[]{:S(2)}) collective-permute-start(bf16[2,96,768]{2,1,0:T(8,128)(2,1)S(1)} %collective-permute-done.8.refs_2_), channel_id=1, source_target_pairs={{0,4},{4,0},{8,12},{12,8},{16,20},{20,16},{24,28},{28,24},{1,5},{5... | collective-permute-start | bytes 884744 | tf_op jit(solution)/shard_map/ppermute | solution.py:224
  72.7 5.7 %collective-permute-start.11 = (bf16[2,96,768]{2,1,0:T(8,128)(2,1)S(1)}, bf16[2,96,768]{2,1,0:T(8,128)(2,1)S(1)}, u32[]{:S(2)}, u32[]{:S(2)}) collective-permute-start(bf16[2,96,768]{2,1,0:T(8,128)(2,1)S(1)} %collective-permute-done.10.refs_4_), channel_id=1, source_target_pairs={{0,4},{4,0},{8,12},{12,8},{16,20},{20,16},{24,28},{28,24},{1,5},{5... | collective-permute-start | bytes 884744 | tf_op jit(solution)/shard_map/ppermute | solution.py:224
  72.7 5.7 %collective-permute-start.13 = (bf16[2,96,768]{2,1,0:T(8,128)(2,1)S(1)}, bf16[2,96,768]{2,1,0:T(8,128)(2,1)S(1)}, u32[]{:S(2)}, u32[]{:S(2)}) collective-permute-start(bf16[2,96,768]{2,1,0:T(8,128)(2,1)S(1)} %collective-permute-done.12.refs_6_), channel_id=1, source_target_pairs={{0,4},{4,0},{8,12},{12,8},{16,20},{20,16},{24,28},{28,24},{1,5},{5... | collective-permute-start | bytes 884744 | tf_op jit(solution)/shard_map/ppermute | solution.py:224
  73.3 1.5 %collective-permute-start.15 = (f32[1,768]{1,0:T(1,128)S(1)}, f32[1,768]{1,0:T(1,128)S(1)}, u32[]{:S(2)}, u32[]{:S(2)}) collective-permute-start(f32[1,768]{1,0:T(1,128)S(1)} %add_add_fusion), channel_id=1, source_target_pairs={{0,4},{4,0},{8,12},{12,8},{16,20},{20,16},{24,28},{28,24},{1,5},{5... | collective-permute-start | bytes 9224 | tf_op jit(solution)/shard_map/ppermute | solution.py:224
  74.9 30.1 %collective-permute-start.16 = (bf16[112,768]{1,0:T(8,128)(2,1)S(1)}, bf16[112,768]{1,0:T(8,128)(2,1)S(1)}, u32[]{:S(2)}, u32[]{:S(2)}) collective-permute-start(bf16[112,768]{1,0:T(8,128)(2,1)S(1)} %get-tuple-element.65), channel_id=1, source_target_pairs={{0,8},{4,12},{8,0},{12,4},{16,24},{20,28},{24,16},{28,20},{1,9},{5... | collective-permute-start | bytes 516104 | tf_op jit(solution)/shard_map/ppermute | solution.py:224
  76.0 29.0 %collective-permute-start.17 = (bf16[112,768]{1,0:T(8,128)(2,1)S(1)}, bf16[112,768]{1,0:T(8,128)(2,1)S(1)}, u32[]{:S(2)}, u32[]{:S(2)}) collective-permute-start(bf16[112,768]{1,0:T(8,128)(2,1)S(1)} %get-tuple-element.64), channel_id=1, source_target_pairs={{0,16},{4,20},{8,24},{12,28},{16,0},{20,4},{24,8},{28,12},{1,17},{... | collective-permute-start | bytes 516104 | tf_op jit(solution)/shard_map/ppermute | solution.py:224
  77.1 28.0 %collective-permute-start.18 = (bf16[112,768]{1,0:T(8,128)(2,1)S(1)}, bf16[112,768]{1,0:T(8,128)(2,1)S(1)}, u32[]{:S(2)}, u32[]{:S(2)}) collective-permute-start(bf16[112,768]{1,0:T(8,128)(2,1)S(1)} %get-tuple-element.63), channel_id=1, source_target_pairs={{0,24},{4,28},{8,16},{12,20},{16,8},{20,12},{24,0},{28,4},{1,25},{... | collective-permute-start | bytes 516104 | tf_op jit(solution)/shard_map/ppermute | solution.py:224
  (8 other events, 20.5 us)
